TPU v7x, 32 devices: a whole 2x2x4 slice. The times are simulated.
32 devices in a mesh: conv: 4 (over y, core), seq: 4 (over z), tensor: 2 (over x).
Axes of the slice: x: 2, y: 2, z: 4, core: 2. Of those that a mesh axis runs over, the one named last changes fastest.
Arguments:
- queries: bfloat16 [4, 512, 4096], P('conv', 'seq', 'tensor'), may hold values from -6 to 6
- keys: bfloat16 [8, 1664, 1024], P('conv', ('seq', 'tensor')), may hold values from -6 to 6
- values: bfloat16 [8, 1664, 1024], P('conv', ('seq', 'tensor')), may hold values from -18 to 18
- q_gain: float32 [128], replicated, may hold values from 0.9 to 2.2
- k_gain: float32 [128], replicated, may hold values from 0.9 to 2.2
- gate: float32 [1], replicated, may hold values from 0.4 to 1.6
- tile_count: int32 [4], replicated, may hold values from 1 to 2, as said below
- tile_owner: int32 [4, 2], replicated, may hold values from -1 to 3, as said below
- visible: int32 [4, 512], replicated, may hold values from 0 to 2, as said below
- d_out: bfloat16 [4, 512, 4096], P('conv', 'seq', 'tensor'), may hold values from -12 to 12
Outputs:
- attended: bfloat16 [4, 512, 4096], P('conv', 'seq', 'tensor')
- d_queries: bfloat16 [4, 512, 4096], P('conv', 'seq', 'tensor')
- d_keys: bfloat16 [8, 1664, 1024], P('conv', ('seq', 'tensor'))
- d_values: bfloat16 [8, 1664, 1024], P('conv', ('seq', 'tensor'))
Inputs may be any that keep to these rules, and one draw needn't show every extreme that they name: `tile_count`: some conversation has 2 tiles. `tile_owner`: entries with t at or past the conversation's count are -1. The tiles of one conversation have different owners, no two tiles share a slot, and some conv index holds 2 tiles. `visible`: never falls along a conversation's text; it is 0 at the first token and 2 at the last.
All inputs are finite; a program needn't handle non-finite values.
Results may differ from a plain program's by a relative error of at most 0.02.
Values may be sent and summed in bfloat16 or wider, within the bound.
A program may use at most 128 MiB of HBM per device.

v0:
```python
from functools import partial
import math

import jax
import jax.numpy as jnp
from jax import lax
from jax.experimental import pallas as pl
from jax.experimental.pallas import tpu as pltpu
from jax.sharding import PartitionSpec as P

TILE = 1601


EPSILON = 1e-05


def head_norm(inputs, norm_gain):
    mean_square = jnp.mean(inputs * inputs, axis=-1, keepdims=True)
    return inputs * lax.rsqrt(mean_square + EPSILON) * norm_gain


def key_mask(seen_tiles, tile_index, row_start, row_count):
    row_ids = row_start + jnp.arange(row_count, dtype=jnp.int32)
    return (seen_tiles > tile_index)[:, None] & (row_ids < TILE)[None, :]


def tile_weights(query_bf, key_tile, visible_keys, score_scale):
    scores = (
        jnp.einsum("pkgd,rkd->kgpr", query_bf, key_tile, preferred_element_type=jnp.float32)
        * score_scale
    )
    return jnp.where(visible_keys[None, None], jnp.exp(scores), 0.0)


def tile_forward(query_bf, key_tile, value_tile, visible_keys, score_scale):
    weights = tile_weights(query_bf, key_tile, visible_keys, score_scale)
    weighted = jnp.einsum(
        "kgpr,rkd->pkgd",
        weights.astype(jnp.bfloat16),
        value_tile,
        preferred_element_type=jnp.float32,
    )
    return (jnp.sum(weights, axis=-1), weighted)


def tile_gradients(
    query_bf,
    grad_bf,
    key_tile,
    value_tile,
    visible_keys,
    safe_sum,
    row_delta,
    score_scale,
    block_count,
):
    weights = tile_weights(query_bf, key_tile, visible_keys, score_scale)
    probability = weights / safe_sum[..., None]
    grad_prob = jnp.einsum(
        "pkgd,rkd->kgpr", grad_bf, value_tile, preferred_element_type=jnp.float32
    )
    grad_score = (probability * (grad_prob - row_delta[..., None])).astype(jnp.bfloat16)
    prob_bf = probability.astype(jnp.bfloat16)
    grad_query = (
        jnp.einsum("kgpr,rkd->pkgd", grad_score, key_tile, preferred_element_type=jnp.float32)
        * score_scale
    )
    kv_local, group_size, token_count, row_count = grad_score.shape
    head_size = query_bf.shape[-1]
    block_tokens = token_count // block_count
    score_blocks = grad_score.reshape(kv_local, group_size, block_count, block_tokens, row_count)
    prob_blocks = prob_bf.reshape(kv_local, group_size, block_count, block_tokens, row_count)
    query_blocks = query_bf.reshape(block_count, block_tokens, kv_local, group_size, head_size)
    grad_blocks = grad_bf.reshape(block_count, block_tokens, kv_local, group_size, head_size)
    key_part = (
        jnp.einsum(
            "kgbpr,bpkgd->brkd", score_blocks, query_blocks, preferred_element_type=jnp.float32
        )
        * score_scale
    )
    value_part = jnp.einsum(
        "kgbpr,bpkgd->brkd", prob_blocks, grad_blocks, preferred_element_type=jnp.float32
    )
    key_part = jnp.sum(
        lax.optimization_barrier(key_part.astype(jnp.bfloat16)).astype(jnp.float32), axis=0
    )
    value_part = jnp.sum(
        lax.optimization_barrier(value_part.astype(jnp.bfloat16)).astype(jnp.float32), axis=0
    )
    return (
        grad_query,
        key_part.reshape(row_count, kv_local * head_size),
        value_part.reshape(row_count, kv_local * head_size),
    )


def attend_forward(query_bf, tile_keys, tile_values, seen_tiles, row_start, score_scale):
    row_count, slot_count, features = tile_keys.shape
    token_count, kv_local, group_size, head_size = query_bf.shape
    weight_sum = jnp.zeros((kv_local, group_size, token_count), jnp.float32)
    weighted = jnp.zeros(query_bf.shape, jnp.float32)
    for tile_index in range(slot_count):
        key_tile = tile_keys[:, tile_index].reshape(row_count, kv_local, head_size)
        value_tile = tile_values[:, tile_index].reshape(row_count, kv_local, head_size)
        visible_keys = key_mask(seen_tiles, tile_index, row_start, row_count)
        work = partial(tile_forward, query_bf, key_tile, value_tile, visible_keys, score_scale)
        part_sum, part_weighted = work()
        weight_sum = weight_sum + part_sum
        weighted = weighted + part_weighted
    return (weight_sum, weighted)


def attend_backward(
    query_bf,
    grad_bf,
    tile_keys,
    tile_values,
    seen_tiles,
    row_start,
    safe_sum,
    row_delta,
    score_scale,
    block_tokens,
):
    row_count, slot_count, features = tile_keys.shape
    token_count, kv_local, group_size, head_size = query_bf.shape
    block_count = token_count // block_tokens
    grad_query = jnp.zeros(query_bf.shape, jnp.float32)
    key_parts = []
    value_parts = []
    for tile_index in range(slot_count):
        key_tile = tile_keys[:, tile_index].reshape(row_count, kv_local, head_size)
        value_tile = tile_values[:, tile_index].reshape(row_count, kv_local, head_size)
        visible_keys = key_mask(seen_tiles, tile_index, row_start, row_count)
        work = partial(
            tile_gradients,
            query_bf,
            grad_bf,
            key_tile,
            value_tile,
            visible_keys,
            safe_sum,
            row_delta,
            score_scale,
            block_count,
        )
        part_query, key_part, value_part = work()
        grad_query = grad_query + part_query
        key_parts.append(key_part)
        value_parts.append(value_part)
    return (grad_query, jnp.stack(key_parts, axis=1), jnp.stack(value_parts, axis=1))


def row_shards(queries, keys, values, q_gain, k_gain, gate, tile_count, tile_owner, visible, d_out):
    conv_count = lax.axis_size("conv")
    tensor_count = lax.axis_size("tensor")
    conv_index = lax.axis_index("conv")
    sequence_index = lax.axis_index("seq")
    slot_count, row_local, features = keys.shape
    head_size = q_gain.shape[0]
    kv_heads = features // head_size
    kv_local = kv_heads // tensor_count
    token_count = queries.shape[1]
    query_heads = queries.shape[2] // head_size
    group_size = query_heads // kv_local
    score_scale = 1.0 / math.sqrt(head_size)
    gate_value = jnp.tanh(gate[0])
    conv_ids = jnp.arange(conv_count, dtype=jnp.int32)
    transfers = (tile_owner == conv_index).astype(jnp.bfloat16)
    own_owners = lax.dynamic_index_in_dim(tile_owner, conv_index, 0, keepdims=False)
    takes = (own_owners[:, None] == conv_ids[None, :]).astype(jnp.bfloat16)
    own_count = lax.dynamic_index_in_dim(tile_count, conv_index, 0, keepdims=False)
    seen_all = jnp.minimum(
        lax.dynamic_index_in_dim(visible, conv_index, 0, keepdims=False), own_count
    )
    key_raw = keys.astype(jnp.float32).reshape(slot_count, row_local, kv_heads, head_size)
    key_normed, key_back = jax.vjp(lambda inputs: head_norm(inputs, k_gain), key_raw)
    key_halfprec = key_normed.astype(jnp.bfloat16).reshape(slot_count, row_local, features)
    outgoing_keys = jnp.einsum(
        "wn,nki->wki", transfers, key_halfprec, preferred_element_type=jnp.float32
    ).astype(jnp.bfloat16)
    send_values = jnp.einsum(
        "wn,nki->wki", transfers, values, preferred_element_type=jnp.float32
    ).astype(jnp.bfloat16)
    got_keys, got_values = (
        lax.all_to_all(
            lax.all_to_all(outgoing_keys, "conv", split_axis=0, concat_axis=0, tiled=True),
            "tensor",
            split_axis=2,
            concat_axis=1,
            tiled=True,
        ),
        lax.all_to_all(
            lax.all_to_all(send_values, "conv", split_axis=0, concat_axis=0, tiled=True),
            "tensor",
            split_axis=2,
            concat_axis=1,
            tiled=True,
        ),
    )
    tile_keys = jnp.einsum(
        "to,orf->rtf", takes, got_keys, preferred_element_type=jnp.float32
    ).astype(jnp.bfloat16)
    tile_values = jnp.einsum(
        "to,orf->rtf", takes, got_values, preferred_element_type=jnp.float32
    ).astype(jnp.bfloat16)
    query_raw = queries[0].astype(jnp.float32).reshape(token_count, query_heads, head_size)
    query_normed, query_back = jax.vjp(lambda inputs: head_norm(inputs, q_gain), query_raw)
    query_bf = query_normed.astype(jnp.bfloat16).reshape(
        token_count, kv_local, group_size, head_size
    )
    grad_bf = (
        (gate_value * d_out[0].astype(jnp.float32))
        .astype(jnp.bfloat16)
        .reshape(token_count, kv_local, group_size, head_size)
    )
    own_start = sequence_index * token_count
    all_queries = lax.all_gather(query_bf, "seq", axis=0, tiled=True)
    all_grads = lax.all_gather(grad_bf, "seq", axis=0, tiled=True)
    share_rows = tile_keys.shape[0]
    row_start = sequence_index * share_rows
    part_sum, part_weighted = attend_forward(
        all_queries, tile_keys, tile_values, seen_all, row_start, score_scale
    )
    all_weighted, all_weight_sum = (
        lax.psum(part_weighted.astype(jnp.bfloat16), "seq").astype(jnp.float32),
        lax.psum(part_sum.astype(jnp.bfloat16), "seq").astype(jnp.float32),
    )
    safe_all = jnp.where(all_weight_sum > 0, all_weight_sum, 1.0)
    context_all = all_weighted / jnp.transpose(safe_all, (2, 0, 1))[..., None]
    context = lax.dynamic_slice_in_dim(context_all, own_start, token_count, 0)
    row_delta = jnp.transpose(
        jnp.sum(all_grads.astype(jnp.float32) * context_all, axis=-1), (1, 2, 0)
    )
    grad_part, key_sums, value_sums = attend_backward(
        all_queries,
        all_grads,
        tile_keys,
        tile_values,
        seen_all,
        row_start,
        safe_all,
        row_delta,
        score_scale,
        token_count,
    )
    grad_query = lax.psum_scatter(
        grad_part.astype(jnp.bfloat16), "seq", scatter_dimension=0, tiled=True
    ).astype(jnp.float32)
    attended = (
        (gate_value * context).astype(jnp.bfloat16).reshape(1, token_count, query_heads * head_size)
    )
    key_round = key_sums.astype(jnp.bfloat16)
    value_round = value_sums.astype(jnp.bfloat16)
    back_keys = jnp.einsum(
        "to,rtf->orf", takes, key_round, preferred_element_type=jnp.float32
    ).astype(jnp.bfloat16)
    back_values = jnp.einsum(
        "to,rtf->orf", takes, value_round, preferred_element_type=jnp.float32
    ).astype(jnp.bfloat16)
    returned_keys, returned_values = (
        lax.all_to_all(
            lax.all_to_all(back_keys, "conv", split_axis=0, concat_axis=0, tiled=True),
            "tensor",
            split_axis=1,
            concat_axis=2,
            tiled=True,
        ),
        lax.all_to_all(
            lax.all_to_all(back_values, "conv", split_axis=0, concat_axis=0, tiled=True),
            "tensor",
            split_axis=1,
            concat_axis=2,
            tiled=True,
        ),
    )
    positioned_keys = jnp.einsum(
        "ew,eig->wig", transfers, returned_keys, preferred_element_type=jnp.float32
    )
    d_values = jnp.einsum(
        "ew,eig->wig", transfers, returned_values, preferred_element_type=jnp.float32
    ).astype(jnp.bfloat16)
    d_keys = key_back(positioned_keys.reshape(slot_count, row_local, kv_heads, head_size))[0]
    d_keys = d_keys.astype(jnp.bfloat16).reshape(slot_count, row_local, features)
    d_queries = query_back(grad_query.reshape(token_count, query_heads, head_size))[0]
    d_queries = d_queries.astype(jnp.bfloat16).reshape(1, token_count, query_heads * head_size)
    return (attended, d_queries, d_keys, d_values)


LOG2E = math.log2(math.e)


def row_chunks(rows):
    starts = list(range(0, max(rows - 511, 1), 512))
    return [(a, b - a) for a, b in zip(starts, starts[1:] + [rows])]


def inverse_rms(inputs):
    return lax.rsqrt(jnp.mean(inputs * inputs, axis=-1, keepdims=True) + EPSILON)


def norm_back(inputs, inv, gained):
    return inv * gained - inputs * (inv * inv * inv) * jnp.mean(
        inputs * gained, axis=-1, keepdims=True
    )


def dot(lhs, rhs):
    return jnp.dot(lhs, rhs, preferred_element_type=jnp.float32)


def prepare_tile(tile, k_raw, v_raw, k_gain, kn, kt, vt):
    rows = k_raw.shape[1]
    for start in range(0, rows, 128):
        at = pl.ds(start, 128)
        raw = k_raw[tile, at, :].astype(jnp.float32)
        normed = raw * inverse_rms(raw) * k_gain
        kn[tile, at, :] = normed.astype(jnp.bfloat16)
        kt[tile, :, at] = normed.T.astype(jnp.bfloat16)
        vt[tile, :, at] = v_raw[tile, at, :].astype(jnp.float32).T.astype(jnp.bfloat16)


def finish_tile(tile, k_raw, k_gain, dk, dv, dk_out, dv_out):
    rows = k_raw.shape[1]
    for start in range(0, rows, 128):
        at = pl.ds(start, 128)
        raw = k_raw[tile, at, :].astype(jnp.float32)
        grad = dk[tile, at, :] * (1.0 / LOG2E) * k_gain
        dk_out[tile, at, :] = norm_back(raw, inverse_rms(raw), grad).astype(jnp.bfloat16)
        dv_out[tile, at, :] = dv[tile, at, :].astype(jnp.bfloat16)


def attend_block(
    block, last_seen, tiles, q_raw, d_out, seen, gate_value, q_gain, v_raw, kn, kt, vt,
    att_out, dq_out, wts, qs, qst, dos, dost, acc, total, dqt, dk, dv,
):
    size = q_gain.shape[1]
    group = q_raw.shape[1] // size
    count = seen.shape[2] // group
    rows = v_raw.shape[1]
    chunks = row_chunks(rows)
    scale = 1.0 / math.sqrt(size)
    at = pl.ds(pl.multiple_of(block * count, count), count)
    for g in range(group):
        raw = q_raw[at, pl.ds(g * size, size)].astype(jnp.float32)
        normed = raw * inverse_rms(raw) * (q_gain * (scale * LOG2E))
        qs[pl.ds(g * count, count), :] = normed.astype(jnp.bfloat16)
        qst[:, pl.ds(g * count, count)] = normed.T.astype(jnp.bfloat16)
    seen_row = seen[block]
    acc[...] = jnp.zeros_like(acc)
    total[...] = jnp.zeros_like(total)
    dqt[...] = jnp.zeros_like(dqt)

    for tile in range(tiles):
        @pl.when(last_seen > tile)
        def _(tile=tile):
            mask = (seen_row > tile).astype(jnp.float32)
            part = jnp.zeros(acc.shape, jnp.float32)
            part_sum = jnp.zeros(total.shape, jnp.float32)
            for start, length in chunks:
                here = pl.ds(start, length)
                w = jnp.exp2(dot(kn[tile, here, :], qst[...]))
                if start + length > TILE:
                    ids = start + lax.broadcasted_iota(jnp.int32, w.shape, 0)
                    w = jnp.where(ids < TILE, w, 0.0)
                part_sum = part_sum + jnp.sum(w, axis=0, keepdims=True)
                w_bf = w.astype(jnp.bfloat16)
                wts[tile, here, :] = w_bf
                part = part + dot(vt[tile, :, here], w_bf)
            acc[...] += part * mask
            total[...] += part_sum * mask

    safe = jnp.where(total[...] > 0, total[...], 1.0)
    inv = 1.0 / safe
    ctx = acc[...] * inv
    for g in range(group):
        lanes = pl.ds(g * count, count)
        grad = d_out[at, pl.ds(g * size, size)].astype(jnp.float32) * gate_value
        dost[:, lanes] = grad.T
        att_out[at, pl.ds(g * size, size)] = (
            (gate_value * ctx[:, g * count:(g + 1) * count]).T.astype(jnp.bfloat16)
        )
    scaled = (dost[...] * inv).astype(jnp.bfloat16)
    scaled32 = scaled.astype(jnp.float32)
    delta = jnp.sum(scaled32 * ctx, axis=0, keepdims=True)

    for tile in range(tiles):
        @pl.when(last_seen > tile)
        def _(tile=tile):
            mask = (seen_row > tile).astype(jnp.float32)
            cut32 = scaled32 * mask
            cut = cut32.astype(jnp.bfloat16)
            for g in range(group):
                dos[pl.ds(g * count, count), :] = (
                    cut32[:, g * count:(g + 1) * count].T.astype(jnp.bfloat16)
                )
            low = delta * mask
            part = jnp.zeros(dqt.shape, jnp.float32)
            for start, length in chunks:
                here = pl.ds(start, length)
                w_bf = wts[tile, here, :]
                dp = dot(v_raw[tile, here, :], cut)
                ds = (w_bf.astype(jnp.float32) * (dp - low)).astype(jnp.bfloat16)
                dv[tile, here, :] += dot(w_bf, dos[...])
                dk[tile, here, :] += dot(ds, qs[...])
                part = part + dot(kt[tile, :, here], ds)
            dqt[...] += part

    for g in range(group):
        raw = q_raw[at, pl.ds(g * size, size)].astype(jnp.float32)
        grad = dqt[:, pl.ds(g * count, count)].T * (q_gain * scale)
        dq_out[at, pl.ds(g * size, size)] = norm_back(raw, inverse_rms(raw), grad).astype(
            jnp.bfloat16
        )


def head_kernel(
    last, counts, gate, q_raw, d_out, k_raw, v_raw, seen, q_gain_ref, k_gain_ref,
    att_out, dq_out, dk_out, dv_out,
    kn, kt, vt, wts, qs, qst, dos, dost, acc, total, dqt, dk, dv,
):
    tiles = k_raw.shape[0]
    q_gain = q_gain_ref[...]
    k_gain = k_gain_ref[...]
    dk[...] = jnp.zeros_like(dk)
    dv[...] = jnp.zeros_like(dv)
    for tile in range(tiles):
        prepare_tile(tile, k_raw, v_raw, k_gain, kn, kt, vt)

    @pl.loop(0, seen.shape[0])
    def _(block):
        attend_block(
            block, last[block], tiles, q_raw, d_out, seen, gate[0], q_gain, v_raw, kn, kt, vt,
            att_out, dq_out, wts, qs, qst, dos, dost, acc, total, dqt, dk, dv,
        )

    for tile in range(tiles):
        finish_tile(tile, k_raw, k_gain, dk, dv, dk_out, dv_out)


def core_scratch(tiles, rows, size, lanes):
    bf, f32 = jnp.bfloat16, jnp.float32
    return [
        pltpu.VMEM((tiles, rows, size), bf),
        pltpu.VMEM((tiles, size, rows), bf),
        pltpu.VMEM((tiles, size, rows), bf),
        pltpu.VMEM((tiles, rows, lanes), bf),
        pltpu.VMEM((lanes, size), bf),
        pltpu.VMEM((size, lanes), bf),
        pltpu.VMEM((lanes, size), bf),
        pltpu.VMEM((size, lanes), f32),
        pltpu.VMEM((size, lanes), f32),
        pltpu.VMEM((1, lanes), f32),
        pltpu.VMEM((size, lanes), f32),
        pltpu.VMEM((tiles, rows, size), f32),
        pltpu.VMEM((tiles, rows, size), f32),
    ]


def move_convs(outgoing):
    count = len(outgoing)
    return [outgoing[0]] + [
        lax.ppermute(outgoing[shift], "conv", [(i, (i + shift) % count) for i in range(count)])
        for shift in range(1, count)
    ]


def choose(arrived, index):
    chosen = arrived[0]
    for shift in range(1, len(arrived)):
        chosen = jnp.where(index == shift, arrived[shift], chosen)
    return chosen


def head_shards(queries, keys, values, q_gain, k_gain, gate, tile_count, tile_owner, visible, d_out):
    conv_count = lax.axis_size("conv")
    tensor_count = lax.axis_size("tensor")
    seq_count = lax.axis_size("seq")
    conv_index = lax.axis_index("conv")
    slot_count, row_local, features = keys.shape
    size = q_gain.shape[0]
    block_tokens, width = queries.shape[1:]
    group = width // (features // tensor_count)
    lanes = group * block_tokens
    everyone = ("conv", "seq", "tensor")

    own_owners = lax.dynamic_index_in_dim(tile_owner, conv_index, 0, keepdims=False)
    own_count = lax.dynamic_index_in_dim(tile_count, conv_index, 0, keepdims=False)
    seen = jnp.minimum(lax.dynamic_index_in_dim(visible, conv_index, 0, keepdims=False), own_count)
    seen = seen.reshape(seq_count, 1, block_tokens)
    last = seen[:, 0, -1]
    seen = jnp.tile(seen, (1, 1, group))

    both = jnp.stack([queries[0], d_out[0]]).reshape(2, block_tokens, seq_count, width // seq_count)
    both = lax.all_to_all(both, "seq", split_axis=2, concat_axis=1, tiled=True)
    both = both.reshape(2, seq_count * block_tokens, width // seq_count)

    goes = tile_owner == conv_index
    slot_of = jnp.argmax(goes, axis=1)
    shifts = list(range(conv_count))
    own_shift = jnp.remainder(conv_index - own_owners, conv_count)

    def fetch(stored):
        outgoing = [
            lax.dynamic_index_in_dim(
                stored, slot_of[jnp.remainder(conv_index + shift, conv_count)], 0, keepdims=False
            )
            for shift in shifts
        ]
        arrived = move_convs(outgoing)
        mine = jnp.stack([choose(arrived, own_shift[tile]) for tile in range(slot_count)])
        mine = mine.reshape(slot_count, row_local, tensor_count, seq_count, size)
        mine = jnp.transpose(mine, (3, 2, 0, 1, 4)).reshape(-1, slot_count, row_local, size)
        mine = lax.all_to_all(mine, ("seq", "tensor"), split_axis=0, concat_axis=0, tiled=True)
        return jnp.transpose(mine, (1, 0, 2, 3)).reshape(slot_count, -1, size)

    key_tiles = fetch(keys)
    value_tiles = fetch(values)
    rows = key_tiles.shape[1]

    vmem = pl.BlockSpec(memory_space=pltpu.VMEM)
    smem = pl.BlockSpec(memory_space=pltpu.SMEM)
    att, dq, dk, dv = pl.pallas_call(
        head_kernel,
        out_shape=[jax.ShapeDtypeStruct(both.shape[1:], jnp.bfloat16)] * 2
        + [jax.ShapeDtypeStruct((slot_count, rows, size), jnp.bfloat16)] * 2,
        in_specs=[smem] * 3 + [vmem] * 7,
        out_specs=[vmem] * 4,
        scratch_shapes=core_scratch(slot_count, rows, size, lanes),
        compiler_params=pltpu.CompilerParams(vmem_limit_bytes=60 << 20),
    )(
        last, own_count.reshape(1), jnp.tanh(gate), both[0], both[1], key_tiles, value_tiles,
        seen, q_gain[None], k_gain[None],
    )

    tile_of = jnp.argmax(own_owners[None, :] == jnp.arange(conv_count)[:, None], axis=1)
    taker = jnp.argmax(goes, axis=0)
    used = jnp.any(goes, axis=0)
    taker_shift = jnp.remainder(conv_index - taker, conv_count)

    def give_back(grads):
        grads = jnp.transpose(grads.reshape(slot_count, -1, row_local, size), (1, 0, 2, 3))
        grads = lax.all_to_all(grads, ("seq", "tensor"), split_axis=0, concat_axis=0, tiled=True)
        grads = grads.reshape(seq_count, tensor_count, slot_count, row_local, size)
        grads = jnp.transpose(grads, (2, 3, 1, 0, 4)).reshape(slot_count, row_local, features)
        outgoing = [
            lax.dynamic_index_in_dim(
                grads, tile_of[jnp.remainder(conv_index + shift, conv_count)], 0, keepdims=False
            )
            for shift in shifts
        ]
        arrived = move_convs(outgoing)
        zero = jnp.zeros((), jnp.bfloat16)
        return jnp.stack(
            [
                jnp.where(used[slot], choose(arrived, taker_shift[slot]), zero)
                for slot in range(slot_count)
            ]
        )

    d_keys = give_back(dk)
    outs = jnp.stack([att, dq])
    outs, d_keys = lax.optimization_barrier((outs, d_keys))
    outs = outs.reshape(2, seq_count, block_tokens, width // seq_count)
    outs = lax.all_to_all(outs, "seq", split_axis=1, concat_axis=3, tiled=True)
    attended = outs[0].reshape(1, block_tokens, width)
    d_queries = outs[1].reshape(1, block_tokens, width)

    return (attended, d_queries, d_keys, give_back(dv))


def shards(queries, keys, *rest):
    heads = keys.shape[2] // rest[1].shape[0]
    split = lax.axis_size("seq") * lax.axis_size("tensor")
    return (head_shards if heads == split else row_shards)(queries, keys, *rest)


def solution(mesh):
    in_specs = (
        P("conv", "seq", "tensor"),
        P("conv", ("seq", "tensor"), None),
        P("conv", ("seq", "tensor"), None),
        P(),
        P(),
        P(),
        P(),
        P(),
        P(),
        P("conv", "seq", "tensor"),
    )
    out_specs = (
        P("conv", "seq", "tensor"),
        P("conv", "seq", "tensor"),
        P("conv", ("seq", "tensor"), None),
        P("conv", ("seq", "tensor"), None),
    )
    return jax.shard_map(shards, mesh=mesh, in_specs=in_specs, out_specs=out_specs, check_vma=False)
```

profile of v0, /device:TPU:9, one launch (start us, length us, event | category | flops | bytes accessed | tf_op | source)
XLA Modules:
  0.0 220.4 jit_solution(4045552178945072713)
XLA Ops:
  0.6 1.4 copy.65
  2.4 1.3 copy.67
  3.7 4.9 %all-to-all-start = ((bf16[2,128,4,512]{3,1,0,2:T(8,128)(2,1)}), bf16[2,128,4,512]{3,1,0,2:T(8,128)(2,1)S(1)}, u32[]{:S(2)}, u32[]{:S(2)}) async-start(bf16[2,128,4,512]{3,1,0,2:T(8,128)(2,1)} %copy.67), calls=%async_computation | async-start | bytes 2097152 | tf_op jit(solution)/shard_map/all_to_all | solution.py:495
  8.6 0.7 copy-done.7
  9.7 0.6 compare_reduce_fusion
  10.8 0.7 fusion.33
  17.3 1.0 dynamic-slice_bitcast_fusion.6
  18.3 1.2 collective-permute-start.3
  19.5 1.2 collective-permute-start.4
  20.8 0.8 collective-permute-start.5
  21.6 0.6 iota_reduce_fusion
  28.4 2.8 %collective-permute-done.3 = bf16[208,1024]{1,0:T(8,128)(2,1)S(1)} collective-permute-done((bf16[208,1024]{1,0:T(8,128)(2,1)}, bf16[208,1024]{1,0:T(8,128)(2,1)S(1)}, u32[]{:S(2)}, u32[]{:S(2)}) %collective-permute-start.3) | collective-permute-done | bytes 426016 | tf_op jit(solution)/shard_map/ppermute | solution.py:463
  31.6 7.5 %collective-permute-done.5 = bf16[208,1024]{1,0:T(8,128)(2,1)} collective-permute-done((bf16[208,1024]{1,0:T(8,128)(2,1)S(1)}, bf16[208,1024]{1,0:T(8,128)(2,1)}, u32[]{:S(2)}, u32[]{:S(2)}) %collective-permute-start.5) | collective-permute-done | bytes 426016 | tf_op jit(solution)/shard_map/ppermute | solution.py:463
  39.1 1.2 fusion.17
  40.9 0.6 maximum_bitcast_fusion
  41.5 1.0 copy.71
  42.5 5.6 %all-to-all-start.2 = ((bf16[8,2,208,128]{3,2,1,0:T(8,128)(2,1)}), bf16[8,2,208,128]{3,2,1,0:T(8,128)(2,1)S(1)}, u32[]{:S(2)}, u32[]{:S(2)}) async-start(bf16[8,2,208,128]{3,2,1,0:T(8,128)(2,1)} %bitcast.167), calls=%async_computation.2 | async-start | bytes 1703936 | tf_op jit(solution)/shard_map/all_to_all | solution.py:514
  48.3 3.3 %collective-permute-start = (bf16[208,1024]{1,0:T(8,128)(2,1)S(1)}, bf16[208,1024]{1,0:T(8,128)(2,1)S(1)}, u32[]{:S(2)}, u32[]{:S(2)}) collective-permute-start(bf16[208,1024]{1,0:T(8,128)(2,1)S(1)} %get-tuple-element.55), channel_id=1, source_target_pairs={{0,24},{8,0},{16,8},{24,16},{1,25},{9,1},{17,9},{25,17},{2,26},{10... | collective-permute-start | bytes 1277960 | tf_op jit(solution)/shard_map/ppermute | solution.py:463
  51.6 1.7 collective-permute-start.2
  53.3 7.6 %collective-permute-done = bf16[208,1024]{1,0:T(8,128)(2,1)S(1)} collective-permute-done((bf16[208,1024]{1,0:T(8,128)(2,1)S(1)}, bf16[208,1024]{1,0:T(8,128)(2,1)S(1)}, u32[]{:S(2)}, u32[]{:S(2)}) %collective-permute-start) | collective-permute-done | bytes 426016 | tf_op jit(solution)/shard_map/ppermute | solution.py:463
  60.9 2.5 %collective-permute-done.1 = bf16[208,1024]{1,0:T(8,128)(2,1)S(1)} collective-permute-done((bf16[208,1024]{1,0:T(8,128)(2,1)S(1)}, bf16[208,1024]{1,0:T(8,128)(2,1)S(1)}, u32[]{:S(2)}, u32[]{:S(2)}) %collective-permute-start.1) | collective-permute-done | bytes 426016 | tf_op jit(solution)/shard_map/ppermute | solution.py:463
  63.4 6.8 %collective-permute-done.2 = bf16[208,1024]{1,0:T(8,128)(2,1)S(1)} collective-permute-done((bf16[208,1024]{1,0:T(8,128)(2,1)S(1)}, bf16[208,1024]{1,0:T(8,128)(2,1)S(1)}, u32[]{:S(2)}, u32[]{:S(2)}) %collective-permute-start.2) | collective-permute-done | bytes 426016 | tf_op jit(solution)/shard_map/ppermute | solution.py:463
  70.2 0.9 fusion.21
  71.0 1.3 stack.49
  72.7 1.0 pad_maximum_fusion.2
  73.7 5.6 %all-to-all-start.1 = ((bf16[8,2,208,128]{3,2,1,0:T(8,128)(2,1)}), bf16[8,2,208,128]{3,2,1,0:T(8,128)(2,1)S(1)}, u32[]{:S(2)}, u32[]{:S(2)}) async-start(bf16[8,2,208,128]{3,2,1,0:T(8,128)(2,1)} %bitcast.24), calls=%async_computation.1 | async-start | bytes 1703936 | tf_op jit(solution)/shard_map/all_to_all | solution.py:514
  79.3 0.6 dynamic_slice.94.counts
  79.9 1.3 fusion.24
  81.3 0.6 copy.81
  82.6 1.0 fusion.30
  83.6 1.0 copy.72
  84.6 13.2 %all-to-all-done.1 = bf16[8,2,208,128]{3,2,1,0:T(8,128)(2,1)S(1)} async-done(((bf16[8,2,208,128]{3,2,1,0:T(8,128)(2,1)}), bf16[8,2,208,128]{3,2,1,0:T(8,128)(2,1)S(1)}, u32[]{:S(2)}, u32[]{:S(2)}) %all-to-all-start.1) | async-done | bytes 852000 | tf_op jit(solution)/shard_map/all_to_all | solution.py:514
  97.7 1.0 copy.70
  99.3 20.6 %shard_map.129 = (bf16[512,512]{1,0:T(8,128)(2,1)}, bf16[512,512]{1,0:T(8,128)(2,1)}, bf16[2,1664,128]{2,1,0:T(8,128)(2,1)}, bf16[2,1664,128]{2,1,0:T(8,128)(2,1)}) custom-call(s32[4]{0:T(128)} %bitcast.185, s32[1]{0:T(128)} %dynamic_slice.94.counts, f32[1]{0:T(128)S(6)} %tanh.3.gate, bf16[512,512]{1,0:T(8,128)(2,1)} %bitcast.177, ...), custom_call_target="tpu_custom_call" | custom-call | tf_op jit(solution)/shard_map/pallas_call | solution.py:523
  119.9 2.1 copy.89
  122.0 7.1 %all-to-all-start.3 = ((bf16[8,2,208,128]{3,2,1,0:T(8,128)(2,1)}), bf16[8,2,208,128]{3,2,1,0:T(8,128)(2,1)S(1)}, u32[]{:S(2)}, u32[]{:S(2)}) async-start(bf16[8,2,208,128]{3,2,1,0:T(8,128)(2,1)} %bitcast.160), calls=%async_computation.3 | async-start | bytes 1703936 | tf_op jit(solution)/shard_map/all_to_all | solution.py:543
  129.1 1.0 copy.87
  130.1 17.7 %all-to-all-done.3 = bf16[8,2,208,128]{3,2,1,0:T(8,128)(2,1)S(1)} async-done(((bf16[8,2,208,128]{3,2,1,0:T(8,128)(2,1)}), bf16[8,2,208,128]{3,2,1,0:T(8,128)(2,1)S(1)}, u32[]{:S(2)}, u32[]{:S(2)}) %all-to-all-start.3) | async-done | bytes 852000 | tf_op jit(solution)/shard_map/all_to_all | solution.py:543
  147.7 5.2 %all-to-all-start.5 = ((bf16[8,2,208,128]{3,2,1,0:T(8,128)(2,1)}), bf16[8,2,208,128]{3,2,1,0:T(8,128)(2,1)S(1)}, u32[]{:S(2)}, u32[]{:S(2)}) async-start(bf16[8,2,208,128]{3,2,1,0:T(8,128)(2,1)} %bitcast.158), calls=%async_computation.5 | async-start | bytes 1703936 | tf_op jit(solution)/shard_map/all_to_all | solution.py:543
  158.5 0.7 copy.88
  159.1 0.6 reshape.121
  159.8 1.1 dynamic-slice_bitcast_fusion.3
  160.8 0.8 collective-permute-start.6
  161.6 3.7 %collective-permute-start.7 = (bf16[208,1024]{1,0:T(8,128)(2,1)}, bf16[208,1024]{1,0:T(8,128)(2,1)}, u32[]{:S(2)}, u32[]{:S(2)}) collective-permute-start(bf16[208,1024]{1,0:T(8,128)(2,1)} %get-tuple-element.48), channel_id=1, source_target_pairs={{0,16},{8,24},{16,0},{24,8},{1,17},{9,25},{17,1},{25,9},{2,18},{10... | collective-permute-start | bytes 1277960 | tf_op jit(solution)/shard_map/ppermute | solution.py:463
  165.4 2.0 collective-permute-start.8
  168.7 0.7 fusion.32
  174.0 0.7 fusion.31
  174.7 1.3 collective-permute-done.7
  176.1 7.8 %collective-permute-done.8 = bf16[208,1024]{1,0:T(8,128)(2,1)} collective-permute-done((bf16[208,1024]{1,0:T(8,128)(2,1)}, bf16[208,1024]{1,0:T(8,128)(2,1)}, u32[]{:S(2)}, u32[]{:S(2)}) %collective-permute-start.8) | collective-permute-done | bytes 426016 | tf_op jit(solution)/shard_map/ppermute | solution.py:463
  183.9 2.6 %fusion.11 = (bf16[1,208,1024]{2,1,0:T(8,128)(2,1)S(1)}, bf16[1,208,1024]{2,1,0:T(8,128)(2,1)S(1)}) fusion(bf16[208,1024]{1,0:T(8,128)(2,1)S(1)} %collective-permute-done.6, bf16[208,1024]{1,0:T(8,128)(2,1)} %collective-permute-done.7, bf16[208,1024]{1,0:T(8,128)(2,1)} %collective-permute-done.8, pred[]{:T(512)} %bitcast.52, pred[]{:T(512)} %bitcast.49, ...), kind=kLoop, calls=%fused_computation.25 | loop fusion | flops 1703936 | bytes 2555916 | tf_op jit(solution)/shard_map/stack | solution.py:554
  186.5 1.0 pad_maximum_fusion.3
  187.4 1.1 copy.75
  188.5 4.5 %all-to-all-start.4 = ((bf16[2,4,128,512]{3,2,0,1:T(8,128)(2,1)}), bf16[2,4,128,512]{3,2,0,1:T(8,128)(2,1)S(1)}, u32[]{:S(2)}, u32[]{:S(2)}) async-start(bf16[2,4,128,512]{3,2,0,1:T(8,128)(2,1)} %copy.75), calls=%async_computation.4 | async-start | bytes 2097152 | tf_op jit(solution)/shard_map/all_to_all | solution.py:565
  193.1 0.7 copy.86
  193.7 0.6 reshape.125
  194.5 3.7 %collective-permute-start.11 = (bf16[208,1024]{1,0:T(8,128)(2,1)S(1)}, bf16[208,1024]{1,0:T(8,128)(2,1)S(1)}, u32[]{:S(2)}, u32[]{:S(2)}) collective-permute-start(bf16[208,1024]{1,0:T(8,128)(2,1)S(1)} %get-tuple-element.44), channel_id=1, source_target_pairs={{0,8},{8,16},{16,24},{24,0},{1,9},{9,17},{17,25},{25,1},{2,10},{10... | collective-permute-start | bytes 1277960 | tf_op jit(solution)/shard_map/ppermute | solution.py:463
  198.5 5.4 %collective-permute-done.10 = bf16[208,1024]{1,0:T(8,128)(2,1)S(1)} collective-permute-done((bf16[208,1024]{1,0:T(8,128)(2,1)S(1)}, bf16[208,1024]{1,0:T(8,128)(2,1)S(1)}, u32[]{:S(2)}, u32[]{:S(2)}) %collective-permute-start.10) | collective-permute-done | bytes 426016 | tf_op jit(solution)/shard_map/ppermute | solution.py:463
  203.9 5.2 %collective-permute-done.11 = bf16[208,1024]{1,0:T(8,128)(2,1)S(1)} collective-permute-done((bf16[208,1024]{1,0:T(8,128)(2,1)S(1)}, bf16[208,1024]{1,0:T(8,128)(2,1)S(1)}, u32[]{:S(2)}, u32[]{:S(2)}) %collective-permute-start.11) | collective-permute-done | bytes 426016 | tf_op jit(solution)/shard_map/ppermute | solution.py:463
  209.1 6.1 %collective-permute-done.9 = bf16[208,1024]{1,0:T(8,128)(2,1)S(1)} collective-permute-done((bf16[208,1024]{1,0:T(8,128)(2,1)S(1)}, bf16[208,1024]{1,0:T(8,128)(2,1)S(1)}, u32[]{:S(2)}, u32[]{:S(2)}) %collective-permute-start.9) | collective-permute-done | bytes 426016 | tf_op jit(solution)/shard_map/ppermute | solution.py:463
  215.2 1.4 fusion.3
  216.6 1.0 pad_maximum_fusion.4
  217.6 0.7 copy.76
  218.3 1.0 copy.79
  219.3 1.0 copy.80
  (44 shorter events, 4.7 us)
Async XLA Ops:
  0.6 1.4 copy-start.3
  3.7 13.6 %copy-start = (bf16[2,208,1024]{2,1,0:T(8,128)(2,1)S(1)}, bf16[2,208,1024]{2,1,0:T(8,128)(2,1)}, u32[]{:S(2)}) copy-start(bf16[2,208,1024]{2,1,0:T(8,128)(2,1)} %param.12) | copy-start | bytes 2555908
  3.7 38.8 %all-to-all-start = ((bf16[2,128,4,512]{3,1,0,2:T(8,128)(2,1)}), bf16[2,128,4,512]{3,1,0,2:T(8,128)(2,1)S(1)}, u32[]{:S(2)}, u32[]{:S(2)}) async-start(bf16[2,128,4,512]{3,1,0,2:T(8,128)(2,1)} %copy.67), calls=%async_computation | async-start | bytes 2097152 | tf_op jit(solution)/shard_map/all_to_all | solution.py:495
  8.6 0.7 copy-start.7
  18.3 12.9 %collective-permute-start.3 = (bf16[208,1024]{1,0:T(8,128)(2,1)}, bf16[208,1024]{1,0:T(8,128)(2,1)S(1)}, u32[]{:S(2)}, u32[]{:S(2)}) collective-permute-start(bf16[208,1024]{1,0:T(8,128)(2,1)} %get-tuple-element.52), channel_id=1, source_target_pairs={{0,24},{8,0},{16,8},{24,16},{1,25},{9,1},{17,9},{25,17},{2,26},{10... | collective-permute-start | bytes 1277960 | tf_op jit(solution)/shard_map/ppermute | solution.py:463
  19.5 12.0 %collective-permute-start.4 = (bf16[208,1024]{1,0:T(8,128)(2,1)}, bf16[208,1024]{1,0:T(8,128)(2,1)S(1)}, u32[]{:S(2)}, u32[]{:S(2)}) collective-permute-start(bf16[208,1024]{1,0:T(8,128)(2,1)} %get-tuple-element.51), channel_id=1, source_target_pairs={{0,16},{8,24},{16,0},{24,8},{1,17},{9,25},{17,1},{25,9},{2,18},{10... | collective-permute-start | bytes 1277960 | tf_op jit(solution)/shard_map/ppermute | solution.py:463
  20.8 18.3 %collective-permute-start.5 = (bf16[208,1024]{1,0:T(8,128)(2,1)S(1)}, bf16[208,1024]{1,0:T(8,128)(2,1)}, u32[]{:S(2)}, u32[]{:S(2)}) collective-permute-start(bf16[208,1024]{1,0:T(8,128)(2,1)S(1)} %get-tuple-element.50), channel_id=1, source_target_pairs={{0,8},{8,16},{16,24},{24,0},{1,9},{9,17},{17,25},{25,1},{2,10},{10... | collective-permute-start | bytes 1277960 | tf_op jit(solution)/shard_map/ppermute | solution.py:463
  31.6 7.5 %copy-start.6 = (bf16[208,1024]{1,0:T(8,128)(2,1)}, bf16[208,1024]{1,0:T(8,128)(2,1)S(1)}, u32[]{:S(2)}) copy-start(bf16[208,1024]{1,0:T(8,128)(2,1)S(1)} %collective-permute-done.4) | copy-start | bytes 1277956
  42.5 5.6 %copy-start.1 = (bf16[2,208,1024]{2,1,0:T(8,128)(2,1)S(1)}, bf16[2,208,1024]{2,1,0:T(8,128)(2,1)}, u32[]{:S(2)}) copy-start(bf16[2,208,1024]{2,1,0:T(8,128)(2,1)} %param.11) | copy-start | bytes 2555908
  42.5 31.2 %all-to-all-start.2 = ((bf16[8,2,208,128]{3,2,1,0:T(8,128)(2,1)}), bf16[8,2,208,128]{3,2,1,0:T(8,128)(2,1)S(1)}, u32[]{:S(2)}, u32[]{:S(2)}) async-start(bf16[8,2,208,128]{3,2,1,0:T(8,128)(2,1)} %bitcast.167), calls=%async_computation.2 | async-start | bytes 1703936 | tf_op jit(solution)/shard_map/all_to_all | solution.py:514
  48.3 12.6 %collective-permute-start = (bf16[208,1024]{1,0:T(8,128)(2,1)S(1)}, bf16[208,1024]{1,0:T(8,128)(2,1)S(1)}, u32[]{:S(2)}, u32[]{:S(2)}) collective-permute-start(bf16[208,1024]{1,0:T(8,128)(2,1)S(1)} %get-tuple-element.55), channel_id=1, source_target_pairs={{0,24},{8,0},{16,8},{24,16},{1,25},{9,1},{17,9},{25,17},{2,26},{10... | collective-permute-start | bytes 1277960 | tf_op jit(solution)/shard_map/ppermute | solution.py:463
  51.5 11.8 %collective-permute-start.1 = (bf16[208,1024]{1,0:T(8,128)(2,1)S(1)}, bf16[208,1024]{1,0:T(8,128)(2,1)S(1)}, u32[]{:S(2)}, u32[]{:S(2)}) collective-permute-start(bf16[208,1024]{1,0:T(8,128)(2,1)S(1)} %get-tuple-element.54), channel_id=1, source_target_pairs={{0,16},{8,24},{16,0},{24,8},{1,17},{9,25},{17,1},{25,9},{2,18},{10... | collective-permute-start | bytes 1277960 | tf_op jit(solution)/shard_map/ppermute | solution.py:463
  51.6 18.6 %collective-permute-start.2 = (bf16[208,1024]{1,0:T(8,128)(2,1)S(1)}, bf16[208,1024]{1,0:T(8,128)(2,1)S(1)}, u32[]{:S(2)}, u32[]{:S(2)}) collective-permute-start(bf16[208,1024]{1,0:T(8,128)(2,1)S(1)} %get-tuple-element.53), channel_id=1, source_target_pairs={{0,8},{8,16},{16,24},{24,0},{1,9},{9,17},{17,25},{25,1},{2,10},{10... | collective-permute-start | bytes 1277960 | tf_op jit(solution)/shard_map/ppermute | solution.py:463
  73.7 5.6 %copy-start.8 = (s32[4]{0:T(128)S(1)}, s32[4]{0:T(128)}, u32[]{:S(2)}) copy-start(s32[4]{0:T(128)} %param.16) | copy-start | bytes 52
  73.7 24.0 %all-to-all-start.1 = ((bf16[8,2,208,128]{3,2,1,0:T(8,128)(2,1)}), bf16[8,2,208,128]{3,2,1,0:T(8,128)(2,1)S(1)}, u32[]{:S(2)}, u32[]{:S(2)}) async-start(bf16[8,2,208,128]{3,2,1,0:T(8,128)(2,1)} %bitcast.24), calls=%async_computation.1 | async-start | bytes 1703936 | tf_op jit(solution)/shard_map/all_to_all | solution.py:514
  122.0 7.1 %copy-start.2 = (bf16[2,1664,128]{2,1,0:T(8,128)(2,1)S(1)}, bf16[2,1664,128]{2,1,0:T(8,128)(2,1)}, u32[]{:S(2)}) copy-start(bf16[2,1664,128]{2,1,0:T(8,128)(2,1)} %get-tuple-element.21) | copy-start | bytes 2555908
  122.0 25.7 %all-to-all-start.3 = ((bf16[8,2,208,128]{3,2,1,0:T(8,128)(2,1)}), bf16[8,2,208,128]{3,2,1,0:T(8,128)(2,1)S(1)}, u32[]{:S(2)}, u32[]{:S(2)}) async-start(bf16[8,2,208,128]{3,2,1,0:T(8,128)(2,1)} %bitcast.160), calls=%async_computation.3 | async-start | bytes 1703936 | tf_op jit(solution)/shard_map/all_to_all | solution.py:543
  147.7 40.8 %all-to-all-start.5 = ((bf16[8,2,208,128]{3,2,1,0:T(8,128)(2,1)}), bf16[8,2,208,128]{3,2,1,0:T(8,128)(2,1)S(1)}, u32[]{:S(2)}, u32[]{:S(2)}) async-start(bf16[8,2,208,128]{3,2,1,0:T(8,128)(2,1)} %bitcast.158), calls=%async_computation.5 | async-start | bytes 1703936 | tf_op jit(solution)/shard_map/all_to_all | solution.py:543
  159.7 14.9 %copy-start.4 = (bf16[512,512]{1,0:T(8,128)(2,1)S(1)}, bf16[512,512]{1,0:T(8,128)(2,1)}, u32[]{:S(2)}) copy-start(bf16[512,512]{1,0:T(8,128)(2,1)} %get-tuple-element.14) | copy-start | bytes 1572868
  159.8 14.9 %copy-start.5 = (bf16[512,512]{1,0:T(8,128)(2,1)S(1)}, bf16[512,512]{1,0:T(8,128)(2,1)}, u32[]{:S(2)}) copy-start(bf16[512,512]{1,0:T(8,128)(2,1)} %get-tuple-element.15) | copy-start | bytes 1572868
  160.8 13.9 %collective-permute-start.6 = (bf16[208,1024]{1,0:T(8,128)(2,1)}, bf16[208,1024]{1,0:T(8,128)(2,1)S(1)}, u32[]{:S(2)}, u32[]{:S(2)}) collective-permute-start(bf16[208,1024]{1,0:T(8,128)(2,1)} %get-tuple-element.49), channel_id=1, source_target_pairs={{0,24},{8,0},{16,8},{24,16},{1,25},{9,1},{17,9},{25,17},{2,26},{10... | collective-permute-start | bytes 1277960 | tf_op jit(solution)/shard_map/ppermute | solution.py:463
  161.6 14.4 %collective-permute-start.7 = (bf16[208,1024]{1,0:T(8,128)(2,1)}, bf16[208,1024]{1,0:T(8,128)(2,1)}, u32[]{:S(2)}, u32[]{:S(2)}) collective-permute-start(bf16[208,1024]{1,0:T(8,128)(2,1)} %get-tuple-element.48), channel_id=1, source_target_pairs={{0,16},{8,24},{16,0},{24,8},{1,17},{9,25},{17,1},{25,9},{2,18},{10... | collective-permute-start | bytes 1277960 | tf_op jit(solution)/shard_map/ppermute | solution.py:463
  165.4 18.5 %collective-permute-start.8 = (bf16[208,1024]{1,0:T(8,128)(2,1)}, bf16[208,1024]{1,0:T(8,128)(2,1)}, u32[]{:S(2)}, u32[]{:S(2)}) collective-permute-start(bf16[208,1024]{1,0:T(8,128)(2,1)} %get-tuple-element.47), channel_id=1, source_target_pairs={{0,8},{8,16},{16,24},{24,0},{1,9},{9,17},{17,25},{25,1},{2,10},{10... | collective-permute-start | bytes 1277960 | tf_op jit(solution)/shard_map/ppermute | solution.py:463
  188.5 29.1 %all-to-all-start.4 = ((bf16[2,4,128,512]{3,2,0,1:T(8,128)(2,1)}), bf16[2,4,128,512]{3,2,0,1:T(8,128)(2,1)S(1)}, u32[]{:S(2)}, u32[]{:S(2)}) async-start(bf16[2,4,128,512]{3,2,0,1:T(8,128)(2,1)} %copy.75), calls=%async_computation.4 | async-start | bytes 2097152 | tf_op jit(solution)/shard_map/all_to_all | solution.py:565
  194.4 9.4 %collective-permute-start.10 = (bf16[208,1024]{1,0:T(8,128)(2,1)S(1)}, bf16[208,1024]{1,0:T(8,128)(2,1)S(1)}, u32[]{:S(2)}, u32[]{:S(2)}) collective-permute-start(bf16[208,1024]{1,0:T(8,128)(2,1)S(1)} %get-tuple-element.45), channel_id=1, source_target_pairs={{0,16},{8,24},{16,0},{24,8},{1,17},{9,25},{17,1},{25,9},{2,18},{10... | collective-permute-start | bytes 1277960 | tf_op jit(solution)/shard_map/ppermute | solution.py:463
  194.5 14.6 %collective-permute-start.11 = (bf16[208,1024]{1,0:T(8,128)(2,1)S(1)}, bf16[208,1024]{1,0:T(8,128)(2,1)S(1)}, u32[]{:S(2)}, u32[]{:S(2)}) collective-permute-start(bf16[208,1024]{1,0:T(8,128)(2,1)S(1)} %get-tuple-element.44), channel_id=1, source_target_pairs={{0,8},{8,16},{16,24},{24,0},{1,9},{9,17},{17,25},{25,1},{2,10},{10... | collective-permute-start | bytes 1277960 | tf_op jit(solution)/shard_map/ppermute | solution.py:463
  198.2 17.0 %collective-permute-start.9 = (bf16[208,1024]{1,0:T(8,128)(2,1)S(1)}, bf16[208,1024]{1,0:T(8,128)(2,1)S(1)}, u32[]{:S(2)}, u32[]{:S(2)}) collective-permute-start(bf16[208,1024]{1,0:T(8,128)(2,1)S(1)} %get-tuple-element.46), channel_id=1, source_target_pairs={{0,24},{8,0},{16,8},{24,16},{1,25},{9,1},{17,9},{25,17},{2,26},{10... | collective-permute-start | bytes 1277960 | tf_op jit(solution)/shard_map/ppermute | solution.py:463
where the time goes:
time: 224 us; the launch traced here: 220 us
  waiting for transfers between devices  84.2 us (38%)
  starting transfers between devices  51.8 us (23%)
  local copies, waits for them, and re-layouts  26.3 us (12%)
  between operations  24.4 us (11%)
  Pallas kernels  20.6 us (9%)
  other arithmetic  13 us (6%)
    ppermute x12, waiting for transfers between devices, move_convs(): lax.ppermute(outgoing[shift], 'conv', [(i, (i + shift) % count) for i in...  53.4 us
    pallas_call x1, Pallas kernels, head_shards(): pl.pallas_call(head_kernel, out_shape=[jax.ShapeDtypeStruct(both.shape[1:...  20.6 us
    ppermute x12, starting transfers between devices, move_convs(): lax.ppermute(outgoing[shift], 'conv', [(i, (i + shift) % count) for i in...  18.9 us
    all_to_all x2, waiting for transfers between devices, give_back(): lax.all_to_all(grads, ('seq', 'tensor'), split_axis=0, concat_axis=0, til...  17.7 us
    all_to_all x2, waiting for transfers between devices, fetch(): lax.all_to_all(mine, ('seq', 'tensor'), split_axis=0, concat_axis=0, tile...  13.2 us
    all_to_all x2, starting transfers between devices, give_back(): lax.all_to_all(grads, ('seq', 'tensor'), split_axis=0, concat_axis=0, til...  12.3 us
    all_to_all x2, starting transfers between devices, fetch(): lax.all_to_all(mine, ('seq', 'tensor'), split_axis=0, concat_axis=0, tile...  11.2 us
    another operation x4, other arithmetic, give_back(): jnp.stack([jnp.where(used[slot], choose(arrived, taker_shift[slot]), zero...  5.94 us
  transfers between devices with their start and end apart: 18, of which 13 were waited for; matrix products, arithmetic and copies ran while one was open for 13% of the time, Pallas kernels for 0%

commit v1 on v0

--- a/solution.py
+++ b/solution.py
@@ -309,51 +309,209 @@
     return jnp.dot(lhs, rhs, preferred_element_type=jnp.float32)
 
 
-def prepare_tile(tile, k_raw, v_raw, k_gain, kn, kt, vt):
-    rows = k_raw.shape[1]
-    for start in range(0, rows, 128):
-        at = pl.ds(start, 128)
-        raw = k_raw[tile, at, :].astype(jnp.float32)
-        normed = raw * inverse_rms(raw) * k_gain
-        kn[tile, at, :] = normed.astype(jnp.bfloat16)
-        kt[tile, :, at] = normed.T.astype(jnp.bfloat16)
-        vt[tile, :, at] = v_raw[tile, at, :].astype(jnp.float32).T.astype(jnp.bfloat16)
-
-
-def finish_tile(tile, k_raw, k_gain, dk, dv, dk_out, dv_out):
-    rows = k_raw.shape[1]
-    for start in range(0, rows, 128):
-        at = pl.ds(start, 128)
-        raw = k_raw[tile, at, :].astype(jnp.float32)
-        grad = dk[tile, at, :] * (1.0 / LOG2E) * k_gain
-        dk_out[tile, at, :] = norm_back(raw, inverse_rms(raw), grad).astype(jnp.bfloat16)
-        dv_out[tile, at, :] = dv[tile, at, :].astype(jnp.bfloat16)
-
-
-def attend_block(
-    block, last_seen, tiles, q_raw, d_out, seen, gate_value, q_gain, v_raw, kn, kt, vt,
-    att_out, dq_out, wts, qs, qst, dos, dost, acc, total, dqt, dk, dv,
+def head_kernel(
+    owners, counts, gate, visible, q_gain_ref, k_gain_ref, q_hbm, do_hbm, k_hbm, v_hbm,
+    att_hbm, dq_hbm, ret_hbm,
+    kv, qa, da, seen, kr, kn, kt, vn, vt, wts, qs, qst, dos, dost, acc, total, dqt, dk, dv,
+    att_st, dq_st, gr, ret,
+    kv_send, kv_recv, own_sem, conv_send, conv_recv, relay_send, relay_recv,
+    q_send, q_recv, own_q_sem, out_send, out_recv, own_out_sem,
+    gr_send, gr_recv, back_send, back_recv, backrelay_send, backrelay_recv, ret_sem,
+    *, conv_count, seq_count, tensor_count,
 ):
-    size = q_gain.shape[1]
-    group = q_raw.shape[1] // size
-    count = seen.shape[2] // group
-    rows = v_raw.shape[1]
+    c = lax.axis_index("conv")
+    z = lax.axis_index("seq")
+    x = lax.axis_index("tensor")
+    tiles, row_local, features = k_hbm.shape
+    size = q_gain_ref.shape[1]
+    rows = kn.shape[1]
+    count = q_hbm.shape[0]
+    width = qa.shape[2]
+    group = width // size
+    heads_side = features // size // tensor_count
+    scale = 1.0 / math.sqrt(size)
+
+    def at(conv, seq, tensor):
+        return {"conv": conv, "seq": seq, "tensor": tensor}
+
+    def remote(src, dst, send, recv, device):
+        return pltpu.make_async_remote_copy(
+            src_ref=src, dst_ref=dst, send_sem=send, recv_sem=recv,
+            device_id=device, device_id_type=pl.DeviceIdType.MESH,
+        )
+
+    partner = c + 1 - 2 * lax.rem(c, 2)
+    siblings = [lax.rem(c + 2 * m, conv_count) for m in range(1, conv_count // 2)]
+    far_first = sorted(range(1, seq_count), key=lambda k: -min(k, seq_count - k))
+    offsets = [(0, e) for e in range(tensor_count)]
+    offsets += [(k, e) for k in far_first for e in range(tensor_count)]
+
+    def target(offset):
+        k, e = offset
+        return lax.rem(z + k, seq_count), lax.rem(x + e, tensor_count)
+
+    def source(offset):
+        k, e = offset
+        return lax.rem(z + seq_count - k, seq_count), lax.rem(x + tensor_count - e, tensor_count)
+
+    def block_rows(seq, tensor):
+        start = (seq * tensor_count + tensor) * row_local
+        return pl.ds(pl.multiple_of(start, 16), row_local)
+
+    def head_lanes(seq, tensor):
+        return pl.ds(pl.multiple_of((tensor * heads_side + seq) * size, size), size)
+
+    def group_lanes(seq):
+        return pl.ds(pl.multiple_of(seq * width, width), width)
+
+    barrier = pltpu.get_barrier_semaphore()
+    peers = [at(c, *target(offset)) for offset in offsets[1:]]
+    peers += [at(other, z, x) for other in [partner] + siblings]
+    for peer in peers:
+        pl.semaphore_signal(barrier, inc=1, device_id=peer, device_id_type=pl.DeviceIdType.MESH)
+    pl.semaphore_wait(barrier, len(peers))
+
+    own_rows = block_rows(z, x)
+    stores = (k_hbm, v_hbm)
+    for j, offset in enumerate(offsets):
+        to = target(offset)
+        for part, store in enumerate(stores):
+            src = store.at[:, :, head_lanes(*to)]
+            dst = kv.at[c, part, :, own_rows, :]
+            if j == 0:
+                pltpu.make_async_copy(src, dst, own_sem.at[part]).start()
+            else:
+                remote(src, dst, kv_send.at[part, j], kv_recv.at[part, j], at(c, *to)).start()
+    for part, (store, into) in enumerate(((q_hbm, qa), (do_hbm, da))):
+        pltpu.make_async_copy(store.at[:, group_lanes(z)], into.at[z], own_q_sem.at[part]).start()
+
+    def q_copy(part, k):
+        store, into = ((q_hbm, qa), (do_hbm, da))[part]
+        to = lax.rem(z + k, seq_count)
+        return remote(
+            store.at[:, group_lanes(to)], into.at[z],
+            q_send.at[part, k], q_recv.at[part, seq_count - k], at(c, to, x),
+        )
+
+    for k in reversed(range(1, seq_count)):
+        for part in range(2):
+            q_copy(part, k).start()
+
+    seen_all = jnp.minimum(visible[pl.ds(c, 1), :], counts[c])
+    for b in range(seq_count):
+        piece = seen_all[:, b * count:(b + 1) * count]
+        seen[b] = jnp.concatenate([piece] * group, axis=1)
+    dk[...] = jnp.zeros_like(dk)
+    dv[...] = jnp.zeros_like(dv)
+    q_gain = q_gain_ref[...]
+    k_gain = k_gain_ref[...]
+    gate_value = jnp.tanh(gate[...])
+
+    def kv_view(j):
+        place = block_rows(*source(offsets[j]))
+        return lambda conv: kv.at[conv, :, :, place, :]
+
+    def spread_start(view, j, send, recv):
+        for n, to in enumerate([partner] + siblings):
+            remote(view(c), view(c), send.at[n, j], recv.at[n, j], at(to, z, x)).start()
+
+    def relay_start(view, j, send, recv, r_send, r_recv):
+        for m, other in enumerate(siblings):
+            came = conv_count // 2 - (m + 1)
+            remote(view(c), view(other), send.at[m + 1, j], recv.at[came, j], at(c, z, x)).wait_recv()
+            remote(view(other), view(other), r_send.at[m, j], r_recv.at[m, j], at(partner, z, x)).start()
+
+    def spread_finish(view, j, send, recv, r_send, r_recv):
+        remote(view(c), view(partner), send.at[0, j], recv.at[0, j], at(partner, z, x)).wait_recv()
+        for n in range(len(siblings) + 1):
+            remote(view(c), view(c), send.at[n, j], recv.at[n, j], at(partner, z, x)).wait_send()
+        for m in range(len(siblings)):
+            far = lax.rem(partner + 2 * (m + 1), conv_count)
+            remote(view(far), view(far), r_send.at[m, j], r_recv.at[m, j], at(partner, z, x)).wait()
+
+    for j, offset in enumerate(offsets):
+        place = block_rows(*source(offset))
+        for part, store in enumerate(stores):
+            dst = kv.at[c, part, :, place, :]
+            src = store.at[:, :, head_lanes(z, x)]
+            if j == 0:
+                pltpu.make_async_copy(src, dst, own_sem.at[part]).wait()
+            else:
+                remote(
+                    src, dst, kv_send.at[part, j], kv_recv.at[part, j], at(c, z, x)
+                ).wait_recv()
+        spread_start(kv_view(j), j, conv_send, conv_recv)
+        if j > 0:
+            relay_start(kv_view(j - 1), j - 1, conv_send, conv_recv, relay_send, relay_recv)
+    last = len(offsets) - 1
+    relay_start(kv_view(last), last, conv_send, conv_recv, relay_send, relay_recv)
+    for j in range(len(offsets)):
+        spread_finish(kv_view(j), j, conv_send, conv_recv, relay_send, relay_recv)
+
+    for tile in range(tiles):
+        owner = owners[c, tile]
+
+        @pl.loop(0, rows // 128)
+        def _(step, tile=tile, owner=owner):
+            here = pl.ds(pl.multiple_of(step * 128, 128), 128)
+
+            def chosen(part):
+                value = kv[0, part, tile, here, :]
+                for conv in range(1, conv_count):
+                    value = jnp.where(owner == conv, kv[conv, part, tile, here, :], value)
+                return value
+
+            raw_bf = chosen(0)
+            raw = raw_bf.astype(jnp.float32)
+            normed = raw * inverse_rms(raw) * k_gain
+            kr[tile, here, :] = raw_bf
+            kn[tile, here, :] = normed.astype(jnp.bfloat16)
+            kt[tile, :, here] = normed.T.astype(jnp.bfloat16)
+            value = chosen(1)
+            vn[tile, here, :] = value
+            vt[tile, :, here] = value.astype(jnp.float32).T.astype(jnp.bfloat16)
+
     chunks = row_chunks(rows)
-    scale = 1.0 / math.sqrt(size)
-    at = pl.ds(pl.multiple_of(block * count, count), count)
-    for g in range(group):
-        raw = q_raw[at, pl.ds(g * size, size)].astype(jnp.float32)
-        normed = raw * inverse_rms(raw) * (q_gain * (scale * LOG2E))
-        qs[pl.ds(g * count, count), :] = normed.astype(jnp.bfloat16)
-        qst[:, pl.ds(g * count, count)] = normed.T.astype(jnp.bfloat16)
-    seen_row = seen[block]
-    acc[...] = jnp.zeros_like(acc)
-    total[...] = jnp.zeros_like(total)
-    dqt[...] = jnp.zeros_like(dqt)
-
-    for tile in range(tiles):
-        @pl.when(last_seen > tile)
-        def _(tile=tile):
+
+    def out_copy(part, i):
+        stage, out = ((att_st, att_hbm), (dq_st, dq_hbm))[part]
+        to = lax.rem(z + i, seq_count)
+        return remote(
+            stage.at[to], out.at[:, group_lanes(z)],
+            out_send.at[part, i], out_recv.at[part, seq_count - i], at(c, to, x),
+        )
+
+    @pl.loop(0, seq_count)
+    def _(i):
+        block = lax.rem(z + i, seq_count)
+
+        @pl.when(i == 0)
+        def _():
+            for part, (store, into) in enumerate(((q_hbm, qa), (do_hbm, da))):
+                pltpu.make_async_copy(
+                    store.at[:, group_lanes(z)], into.at[z], own_q_sem.at[part]
+                ).wait()
+
+        @pl.when(i > 0)
+        def _():
+            for part, (store, into) in enumerate(((q_hbm, qa), (do_hbm, da))):
+                remote(
+                    store.at[:, group_lanes(z)], into.at[block],
+                    q_send.at[part, i], q_recv.at[part, i], at(c, block, x),
+                ).wait_recv()
+
+        for g in range(group):
+            raw = qa[block, :, pl.ds(g * size, size)].astype(jnp.float32)
+            normed = raw * inverse_rms(raw) * (q_gain * (scale * LOG2E))
+            qs[pl.ds(g * count, count), :] = normed.astype(jnp.bfloat16)
+            qst[:, pl.ds(g * count, count)] = normed.T.astype(jnp.bfloat16)
+        seen_row = seen[block]
+        acc[...] = jnp.zeros_like(acc)
+        total[...] = jnp.zeros_like(total)
+        dqt[...] = jnp.zeros_like(dqt)
+
+        @pl.loop(0, tiles)
+        def _(tile):
             mask = (seen_row > tile).astype(jnp.float32)
             part = jnp.zeros(acc.shape, jnp.float32)
             part_sum = jnp.zeros(total.shape, jnp.float32)
@@ -370,23 +528,27 @@
             acc[...] += part * mask
             total[...] += part_sum * mask
 
-    safe = jnp.where(total[...] > 0, total[...], 1.0)
-    inv = 1.0 / safe
-    ctx = acc[...] * inv
-    for g in range(group):
-        lanes = pl.ds(g * count, count)
-        grad = d_out[at, pl.ds(g * size, size)].astype(jnp.float32) * gate_value
-        dost[:, lanes] = grad.T
-        att_out[at, pl.ds(g * size, size)] = (
-            (gate_value * ctx[:, g * count:(g + 1) * count]).T.astype(jnp.bfloat16)
-        )
-    scaled = (dost[...] * inv).astype(jnp.bfloat16)
-    scaled32 = scaled.astype(jnp.float32)
-    delta = jnp.sum(scaled32 * ctx, axis=0, keepdims=True)
-
-    for tile in range(tiles):
-        @pl.when(last_seen > tile)
-        def _(tile=tile):
+        @pl.when(i > 1)
+        def _():
+            for part in range(2):
+                out_copy(part, i - 1).start()
+
+        safe = jnp.where(total[...] > 0, total[...], 1.0)
+        inv = 1.0 / safe
+        ctx = acc[...] * inv
+        for g in range(group):
+            lanes = pl.ds(g * count, count)
+            grad = da[block, :, pl.ds(g * size, size)].astype(jnp.float32) * gate_value
+            dost[:, lanes] = grad.T
+            att_st[block, :, pl.ds(g * size, size)] = (
+                (gate_value * ctx[:, g * count:(g + 1) * count]).T.astype(jnp.bfloat16)
+            )
+        scaled = (dost[...] * inv).astype(jnp.bfloat16)
+        scaled32 = scaled.astype(jnp.float32)
+        delta = jnp.sum(scaled32 * ctx, axis=0, keepdims=True)
+
+        @pl.loop(0, tiles)
+        def _(tile):
             mask = (seen_row > tile).astype(jnp.float32)
             cut32 = scaled32 * mask
             cut = cut32.astype(jnp.bfloat16)
@@ -399,77 +561,96 @@
             for start, length in chunks:
                 here = pl.ds(start, length)
                 w_bf = wts[tile, here, :]
-                dp = dot(v_raw[tile, here, :], cut)
+                dp = dot(vn[tile, here, :], cut)
                 ds = (w_bf.astype(jnp.float32) * (dp - low)).astype(jnp.bfloat16)
                 dv[tile, here, :] += dot(w_bf, dos[...])
                 dk[tile, here, :] += dot(ds, qs[...])
                 part = part + dot(kt[tile, :, here], ds)
             dqt[...] += part
 
-    for g in range(group):
-        raw = q_raw[at, pl.ds(g * size, size)].astype(jnp.float32)
-        grad = dqt[:, pl.ds(g * count, count)].T * (q_gain * scale)
-        dq_out[at, pl.ds(g * size, size)] = norm_back(raw, inverse_rms(raw), grad).astype(
-            jnp.bfloat16
+        for g in range(group):
+            raw = qa[block, :, pl.ds(g * size, size)].astype(jnp.float32)
+            grad = dqt[:, pl.ds(g * count, count)].T * (q_gain * scale)
+            dq_st[block, :, pl.ds(g * size, size)] = norm_back(
+                raw, inverse_rms(raw), grad
+            ).astype(jnp.bfloat16)
+
+    def gr_copy(j):
+        to = target(offsets[j])
+        return remote(
+            gr.at[:, :, block_rows(*to), :], ret.at[c, :, :, :, head_lanes(z, x)],
+            gr_send.at[j], gr_recv.at[j], at(c, *to),
         )
 
-
-def head_kernel(
-    last, counts, gate, q_raw, d_out, k_raw, v_raw, seen, q_gain_ref, k_gain_ref,
-    att_out, dq_out, dk_out, dv_out,
-    kn, kt, vt, wts, qs, qst, dos, dost, acc, total, dqt, dk, dv,
-):
-    tiles = k_raw.shape[0]
-    q_gain = q_gain_ref[...]
-    k_gain = k_gain_ref[...]
-    dk[...] = jnp.zeros_like(dk)
-    dv[...] = jnp.zeros_like(dv)
-    for tile in range(tiles):
-        prepare_tile(tile, k_raw, v_raw, k_gain, kn, kt, vt)
-
-    @pl.loop(0, seen.shape[0])
-    def _(block):
-        attend_block(
-            block, last[block], tiles, q_raw, d_out, seen, gate[0], q_gain, v_raw, kn, kt, vt,
-            att_out, dq_out, wts, qs, qst, dos, dost, acc, total, dqt, dk, dv,
+    order = list(range(2, len(offsets))) + [1, 0]
+    for n, j in enumerate(order):
+        place = block_rows(*target(offsets[j]))
+
+        @pl.loop(0, tiles)
+        def _(tile, place=place):
+            raw = kr[tile, place, :].astype(jnp.float32)
+            grad = dk[tile, place, :] * (1.0 / LOG2E) * k_gain
+            gr[0, tile, place, :] = norm_back(raw, inverse_rms(raw), grad).astype(jnp.bfloat16)
+            gr[1, tile, place, :] = dv[tile, place, :].astype(jnp.bfloat16)
+
+        if n > 0:
+            gr_copy(order[n - 1]).start()
+    for part in range(2):
+        out_copy(part, seq_count - 1).start()
+    stages = ((att_st, att_hbm), (dq_st, dq_hbm))
+    for part, (stage, out) in enumerate(stages):
+        pltpu.make_async_copy(stage.at[z], out.at[:, group_lanes(z)], own_out_sem.at[part]).start()
+    ret[c, :, :, :, head_lanes(z, x)] = gr[:, :, own_rows, :]
+
+    def ret_view(j):
+        lanes = head_lanes(*source(offsets[j]))
+        return lambda conv: ret.at[conv, :, :, :, lanes]
+
+    def ret_out(j):
+        lanes = head_lanes(*source(offsets[j]))
+        return pltpu.make_async_copy(
+            ret.at[:, :, :, :, lanes], ret_hbm.at[:, :, :, :, lanes], ret_sem.at[j]
         )
 
-    for tile in range(tiles):
-        finish_tile(tile, k_raw, k_gain, dk, dv, dk_out, dv_out)
-
-
-def core_scratch(tiles, rows, size, lanes):
-    bf, f32 = jnp.bfloat16, jnp.float32
-    return [
-        pltpu.VMEM((tiles, rows, size), bf),
-        pltpu.VMEM((tiles, size, rows), bf),
-        pltpu.VMEM((tiles, size, rows), bf),
-        pltpu.VMEM((tiles, rows, lanes), bf),
-        pltpu.VMEM((lanes, size), bf),
-        pltpu.VMEM((size, lanes), bf),
-        pltpu.VMEM((lanes, size), bf),
-        pltpu.VMEM((size, lanes), f32),
-        pltpu.VMEM((size, lanes), f32),
-        pltpu.VMEM((1, lanes), f32),
-        pltpu.VMEM((size, lanes), f32),
-        pltpu.VMEM((tiles, rows, size), f32),
-        pltpu.VMEM((tiles, rows, size), f32),
-    ]
-
-
-def move_convs(outgoing):
-    count = len(outgoing)
-    return [outgoing[0]] + [
-        lax.ppermute(outgoing[shift], "conv", [(i, (i + shift) % count) for i in range(count)])
-        for shift in range(1, count)
-    ]
-
-
-def choose(arrived, index):
-    chosen = arrived[0]
-    for shift in range(1, len(arrived)):
-        chosen = jnp.where(index == shift, arrived[shift], chosen)
-    return chosen
+    sems = (back_send, back_recv, backrelay_send, backrelay_recv)
+    arrival = [1] + list(range(2, len(offsets)))
+    arrival = list(range(2, 3)) + [0, 1] + list(range(3, len(offsets)))
+    for n, j in enumerate(arrival):
+        if j > 0:
+            remote(
+                gr.at[:, :, own_rows, :], ret_view(j)(c), gr_send.at[j], gr_recv.at[j], at(c, z, x)
+            ).wait_recv()
+        spread_start(ret_view(j), j, back_send, back_recv)
+        if n > 0:
+            relay_start(ret_view(arrival[n - 1]), arrival[n - 1], *sems)
+        if n > 1:
+            spread_finish(ret_view(arrival[n - 2]), arrival[n - 2], *sems)
+            ret_out(arrival[n - 2]).start()
+    relay_start(ret_view(arrival[-1]), arrival[-1], *sems)
+    for j in arrival[-2:]:
+        spread_finish(ret_view(j), j, *sems)
+        ret_out(j).start()
+
+    for part, (stage, out) in enumerate(stages):
+        for i in range(1, seq_count):
+            remote(
+                stage.at[z], out.at[:, group_lanes(lax.rem(z + seq_count - i, seq_count))],
+                out_send.at[part, i], out_recv.at[part, i], at(c, z, x),
+            ).wait()
+        pltpu.make_async_copy(stage.at[z], out.at[:, group_lanes(z)], own_out_sem.at[part]).wait()
+    for j in range(1, len(offsets)):
+        gr_copy(j).wait_send()
+        for part, store in enumerate(stores):
+            to = target(offsets[j])
+            remote(
+                store.at[:, :, head_lanes(*to)], kv.at[c, part, :, own_rows, :],
+                kv_send.at[part, j], kv_recv.at[part, j], at(c, *to),
+            ).wait_send()
+    for k in range(1, seq_count):
+        for part in range(2):
+            q_copy(part, k).wait_send()
+    for j in range(len(offsets)):
+        ret_out(j).wait()
 
 
 def head_shards(queries, keys, values, q_gain, k_gain, gate, tile_count, tile_owner, visible, d_out):
@@ -479,100 +660,94 @@
     conv_index = lax.axis_index("conv")
     slot_count, row_local, features = keys.shape
     size = q_gain.shape[0]
-    block_tokens, width = queries.shape[1:]
-    group = width // (features // tensor_count)
-    lanes = group * block_tokens
-    everyone = ("conv", "seq", "tensor")
-
-    own_owners = lax.dynamic_index_in_dim(tile_owner, conv_index, 0, keepdims=False)
-    own_count = lax.dynamic_index_in_dim(tile_count, conv_index, 0, keepdims=False)
-    seen = jnp.minimum(lax.dynamic_index_in_dim(visible, conv_index, 0, keepdims=False), own_count)
-    seen = seen.reshape(seq_count, 1, block_tokens)
-    last = seen[:, 0, -1]
-    seen = jnp.tile(seen, (1, 1, group))
-
-    both = jnp.stack([queries[0], d_out[0]]).reshape(2, block_tokens, seq_count, width // seq_count)
-    both = lax.all_to_all(both, "seq", split_axis=2, concat_axis=1, tiled=True)
-    both = both.reshape(2, seq_count * block_tokens, width // seq_count)
-
-    goes = tile_owner == conv_index
-    slot_of = jnp.argmax(goes, axis=1)
-    shifts = list(range(conv_count))
-    own_shift = jnp.remainder(conv_index - own_owners, conv_count)
-
-    def fetch(stored):
-        outgoing = [
-            lax.dynamic_index_in_dim(
-                stored, slot_of[jnp.remainder(conv_index + shift, conv_count)], 0, keepdims=False
-            )
-            for shift in shifts
-        ]
-        arrived = move_convs(outgoing)
-        mine = jnp.stack([choose(arrived, own_shift[tile]) for tile in range(slot_count)])
-        mine = mine.reshape(slot_count, row_local, tensor_count, seq_count, size)
-        mine = jnp.transpose(mine, (3, 2, 0, 1, 4)).reshape(-1, slot_count, row_local, size)
-        mine = lax.all_to_all(mine, ("seq", "tensor"), split_axis=0, concat_axis=0, tiled=True)
-        return jnp.transpose(mine, (1, 0, 2, 3)).reshape(slot_count, -1, size)
-
-    key_tiles = fetch(keys)
-    value_tiles = fetch(values)
-    rows = key_tiles.shape[1]
+    block_tokens, width_all = queries.shape[1:]
+    width = width_all // seq_count
+    lanes = width // size * block_tokens
+    rows = row_local * seq_count * tensor_count
+    bf, f32 = jnp.bfloat16, jnp.float32
+    parts = seq_count * tensor_count
+    far = conv_count // 2 - 1
+    dma = pltpu.SemaphoreType.DMA
 
     vmem = pl.BlockSpec(memory_space=pltpu.VMEM)
     smem = pl.BlockSpec(memory_space=pltpu.SMEM)
-    att, dq, dk, dv = pl.pallas_call(
-        head_kernel,
-        out_shape=[jax.ShapeDtypeStruct(both.shape[1:], jnp.bfloat16)] * 2
-        + [jax.ShapeDtypeStruct((slot_count, rows, size), jnp.bfloat16)] * 2,
-        in_specs=[smem] * 3 + [vmem] * 7,
-        out_specs=[vmem] * 4,
-        scratch_shapes=core_scratch(slot_count, rows, size, lanes),
-        compiler_params=pltpu.CompilerParams(vmem_limit_bytes=60 << 20),
+    hbm = pl.BlockSpec(memory_space=pl.ANY)
+    att, dq, ret = pl.pallas_call(
+        partial(
+            head_kernel, conv_count=conv_count, seq_count=seq_count, tensor_count=tensor_count
+        ),
+        out_shape=[jax.ShapeDtypeStruct((block_tokens, width_all), bf)] * 2
+        + [jax.ShapeDtypeStruct((conv_count, 2, slot_count, row_local, features), bf)],
+        in_specs=[smem] * 2 + [vmem] * 4 + [hbm] * 4,
+        out_specs=[hbm] * 3,
+        scratch_shapes=[
+            pltpu.VMEM((conv_count, 2, slot_count, rows, size), bf),
+            pltpu.VMEM((seq_count, block_tokens, width), bf),
+            pltpu.VMEM((seq_count, block_tokens, width), bf),
+            pltpu.VMEM((seq_count, 1, lanes), jnp.int32),
+            pltpu.VMEM((slot_count, rows, size), bf),
+            pltpu.VMEM((slot_count, rows, size), bf),
+            pltpu.VMEM((slot_count, size, rows), bf),
+            pltpu.VMEM((slot_count, rows, size), bf),
+            pltpu.VMEM((slot_count, size, rows), bf),
+            pltpu.VMEM((slot_count, rows, lanes), bf),
+            pltpu.VMEM((lanes, size), bf),
+            pltpu.VMEM((size, lanes), bf),
+            pltpu.VMEM((lanes, size), bf),
+            pltpu.VMEM((size, lanes), f32),
+            pltpu.VMEM((size, lanes), f32),
+            pltpu.VMEM((1, lanes), f32),
+            pltpu.VMEM((size, lanes), f32),
+            pltpu.VMEM((slot_count, rows, size), f32),
+            pltpu.VMEM((slot_count, rows, size), f32),
+            pltpu.VMEM((seq_count, block_tokens, width), bf),
+            pltpu.VMEM((seq_count, block_tokens, width), bf),
+            pltpu.VMEM((2, slot_count, rows, size), bf),
+            pltpu.VMEM((conv_count, 2, slot_count, row_local, features), bf),
+            dma((2, parts)), dma((2, parts)), dma((2,)),
+            dma((far + 1, parts)), dma((far + 1, parts)), dma((far, parts)), dma((far, parts)),
+            dma((2, seq_count)), dma((2, seq_count)), dma((2,)),
+            dma((2, seq_count)), dma((2, seq_count)), dma((2,)),
+            dma((parts,)), dma((parts,)),
+            dma((far + 1, parts)), dma((far + 1, parts)), dma((far, parts)), dma((far, parts)),
+            dma((parts,)),
+        ],
+        compiler_params=pltpu.CompilerParams(
+            collective_id=0, has_side_effects=True, vmem_limit_bytes=60 << 20
+        ),
     )(
-        last, own_count.reshape(1), jnp.tanh(gate), both[0], both[1], key_tiles, value_tiles,
-        seen, q_gain[None], k_gain[None],
-    )
-
-    tile_of = jnp.argmax(own_owners[None, :] == jnp.arange(conv_count)[:, None], axis=1)
+        tile_owner, tile_count, gate.reshape(1, 1), visible, q_gain[None], k_gain[None],
+        queries[0], d_out[0], keys, values,
+    )
+
+    goes = tile_owner == conv_index
     taker = jnp.argmax(goes, axis=0)
     used = jnp.any(goes, axis=0)
-    taker_shift = jnp.remainder(conv_index - taker, conv_count)
-
-    def give_back(grads):
-        grads = jnp.transpose(grads.reshape(slot_count, -1, row_local, size), (1, 0, 2, 3))
-        grads = lax.all_to_all(grads, ("seq", "tensor"), split_axis=0, concat_axis=0, tiled=True)
-        grads = grads.reshape(seq_count, tensor_count, slot_count, row_local, size)
-        grads = jnp.transpose(grads, (2, 3, 1, 0, 4)).reshape(slot_count, row_local, features)
-        outgoing = [
-            lax.dynamic_index_in_dim(
-                grads, tile_of[jnp.remainder(conv_index + shift, conv_count)], 0, keepdims=False
-            )
-            for shift in shifts
-        ]
-        arrived = move_convs(outgoing)
-        zero = jnp.zeros((), jnp.bfloat16)
+    zero = jnp.zeros((), bf)
+
+    def placed(part):
         return jnp.stack(
             [
-                jnp.where(used[slot], choose(arrived, taker_shift[slot]), zero)
+                jnp.where(
+                    used[slot],
+                    lax.dynamic_index_in_dim(ret[:, part, slot], taker[slot], 0, keepdims=False),
+                    zero,
+                )
                 for slot in range(slot_count)
             ]
         )
 
-    d_keys = give_back(dk)
-    outs = jnp.stack([att, dq])
-    outs, d_keys = lax.optimization_barrier((outs, d_keys))
-    outs = outs.reshape(2, seq_count, block_tokens, width // seq_count)
-    outs = lax.all_to_all(outs, "seq", split_axis=1, concat_axis=3, tiled=True)
-    attended = outs[0].reshape(1, block_tokens, width)
-    d_queries = outs[1].reshape(1, block_tokens, width)
-
-    return (attended, d_queries, d_keys, give_back(dv))
+    return (att[None], dq[None], placed(0), placed(1))
 
 
 def shards(queries, keys, *rest):
     heads = keys.shape[2] // rest[1].shape[0]
-    split = lax.axis_size("seq") * lax.axis_size("tensor")
-    return (head_shards if heads == split else row_shards)(queries, keys, *rest)
+    seq_count, tensor_count = lax.axis_size("seq"), lax.axis_size("tensor")
+    conv_count = lax.axis_size("conv")
+    split = seq_count * tensor_count
+    fits = heads == split and conv_count % 2 == 0 and conv_count > 2
+    fits = fits and keys.shape[1] * split % 128 == 0
+    return (head_shards if fits else row_shards)(queries, keys, *rest)
 
 
 def solution(mesh):

time: 224 us -> 194 us (0.87)
  the two profiles are of different devices: /device:TPU:9 before, /device:TPU:31 now
where the time goes in v1:
time: 194 us; the launch traced here: 193 us
  Pallas kernels  171 us (88%)
  local copies, waits for them, and re-layouts  9.96 us (5%)
  other arithmetic  6.61 us (3%)
  between operations  5.21 us (3%)
    pallas_call x1, Pallas kernels, head_shards(): pl.pallas_call(partial(head_kernel, conv_count=conv_count, seq_count=seq_...  171 us
    slice x1, local copies, waits for them, and re-layouts, placed(): ret[:, part, slot]  5.85 us
    select_n x2, other arithmetic, placed(): jnp.where(used[slot], lax.dynamic_index_in_dim(ret[:, part, slot], taker[...  3.9 us

profile of v1, /device:TPU:31, one launch (start us, length us, event | category | flops | bytes accessed | tf_op | source)
XLA Modules:
  0.0 193.2 jit_solution(17347666286429904940)
XLA Ops:
  0.6 1.3 copy.14.owners
  2.6 171.4 %shard_map.129 = (bf16[128,2048]{1,0:T(8,128)(2,1)}, bf16[128,2048]{1,0:T(8,128)(2,1)}, bf16[4,2,2,208,1024]{4,3,2,1,0:T(8,128)(2,1)}) custom-call(s32[4,2]{1,0:T(4,128)} %copy.14.owners, s32[4]{0:T(128)} %counts.1, f32[1,1]{1,0:T(1,128)} %bitcast.19.gate, s32[4,512]{1,0:T(4,128)} %visible.1, f32[1,128]{1,0:T(1,128)} %bitcast.24, f32[1,128]{1,0:T(1,128)} %bitcast.25, ...), custom_call_target="tpu_custom_call" | custom-call | tf_op jit(solution)/shard_map/pallas_call | solution.py:675
  174.0 0.0 copy-start.2
  174.0 5.9 %fusion.1 = (bf16[4,1,1,208,1024]{4,3,2,1,0:T(8,128)(2,1)S(1)}, bf16[4,1,1,208,1024]{4,3,2,1,0:T(8,128)(2,1)S(1)}, bf16[4,1,1,208,1024]{4,3,2,1,0:T(8,128)(2,1)}, bf16[4,1,1,208,1024]{4,3,2,1,0:T(8,128)(2,1)}) fusion(bf16[4,2,2,208,1024]{4,3,2,1,0:T(8,128)(2,1)} %get-tuple-element.10), kind=kLoop, calls=%fused_computation.9 | loop fusion | bytes 13631488 | tf_op jit(solution)/shard_map/slice | solution.py:733
  179.9 0.0 copy-done.2
  179.9 0.6 iota_reduce_fusion
  180.5 0.6 fusion.3
  183.0 0.1 fusion
  183.2 0.6 fusion.2
  185.7 2.5 %select_bitcast_fusion.2 = (bf16[1,208,1024]{2,1,0:T(8,128)(2,1)S(1)}, bf16[1,208,1024]{2,1,0:T(8,128)(2,1)S(1)}) fusion(bf16[4,1,1,208,1024]{4,3,2,1,0:T(8,128)(2,1)} %get-tuple-element.14, s32[]{:T(128)S(6)} %select_n.80, pred[]{:T(512)} %bitcast.10, bf16[4,1,1,208,1024]{4,3,2,1,0:T(8,128)(2,1)} %get-tuple-element.15, s32[]{:T(128)S(6)} %select_n.76, ...), kind=kLoop, calls=%fused_computation.4 | loop fusion | flops 425984 | bytes 1703946 | tf_op jit(solution)/shard_map/jit(_where)/select_n | solution.py:731
  188.2 1.0 pad_maximum_fusion
  189.2 0.0 copy-start.1
  189.2 1.4 select_bitcast_fusion
  190.6 0.0 copy-start
  190.6 1.0 pad_maximum_fusion.1
  191.6 0.0 copy-done.1
  191.6 0.8 copy.18
  192.4 0.0 copy-done
  192.4 0.8 copy.19
Async XLA Ops:
  174.0 5.9 %copy-start.2 = (s32[4,2]{0,1:T(2,128)S(1)}, s32[4,2]{0,1:T(2,128)}, u32[]{:S(2)}) copy-start(s32[4,2]{0,1:T(2,128)} %param.17) | copy-start | bytes 100
  189.2 2.4 %copy-start.1 = (bf16[128,2048]{1,0:T(8,128)(2,1)S(1)}, bf16[128,2048]{1,0:T(8,128)(2,1)}, u32[]{:S(2)}) copy-start(bf16[128,2048]{1,0:T(8,128)(2,1)} %get-tuple-element.8) | copy-start | bytes 1572868
  190.6 1.8 copy-start

commit v2 on v0

--- a/solution.py
+++ b/solution.py
@@ -290,11 +290,6 @@
 LOG2E = math.log2(math.e)
 
 
-def row_chunks(rows):
-    starts = list(range(0, max(rows - 511, 1), 512))
-    return [(a, b - a) for a, b in zip(starts, starts[1:] + [rows])]
-
-
 def inverse_rms(inputs):
     return lax.rsqrt(jnp.mean(inputs * inputs, axis=-1, keepdims=True) + EPSILON)
 
@@ -309,270 +304,462 @@
     return jnp.dot(lhs, rhs, preferred_element_type=jnp.float32)
 
 
-def prepare_tile(tile, k_raw, v_raw, k_gain, kn, kt, vt):
-    rows = k_raw.shape[1]
-    for start in range(0, rows, 128):
-        at = pl.ds(start, 128)
-        raw = k_raw[tile, at, :].astype(jnp.float32)
-        normed = raw * inverse_rms(raw) * k_gain
-        kn[tile, at, :] = normed.astype(jnp.bfloat16)
-        kt[tile, :, at] = normed.T.astype(jnp.bfloat16)
-        vt[tile, :, at] = v_raw[tile, at, :].astype(jnp.float32).T.astype(jnp.bfloat16)
-
-
-def finish_tile(tile, k_raw, k_gain, dk, dv, dk_out, dv_out):
-    rows = k_raw.shape[1]
-    for start in range(0, rows, 128):
-        at = pl.ds(start, 128)
-        raw = k_raw[tile, at, :].astype(jnp.float32)
-        grad = dk[tile, at, :] * (1.0 / LOG2E) * k_gain
-        dk_out[tile, at, :] = norm_back(raw, inverse_rms(raw), grad).astype(jnp.bfloat16)
-        dv_out[tile, at, :] = dv[tile, at, :].astype(jnp.bfloat16)
-
-
-def attend_block(
-    block, last_seen, tiles, q_raw, d_out, seen, gate_value, q_gain, v_raw, kn, kt, vt,
-    att_out, dq_out, wts, qs, qst, dos, dost, acc, total, dqt, dk, dv,
+def head_kernel(
+    owners, counts, gate, visible, q_gain_ref, k_gain_ref, q_hbm, do_hbm, k_hbm, v_hbm,
+    att_hbm, dq_hbm, dk_hbm, dv_hbm,
+    raw, sel, kvc, qa, da, seen, kn, kt, vt, wts, qs, qst, dt, acc, total, scaled_t, dos, delta,
+    dqt, dk, dv, att_st, dq_st, grads, gsel,
+    own_sem, conv_send, conv_recv, relay_send, relay_recv, kv_send, kv_recv,
+    q_send, q_recv, own_q_sem, out_send, out_recv, own_out_sem,
+    back_send, back_recv, backrelay_send, backrelay_recv, ret_send, ret_recv, own_ret_sem,
+    *, conv_count, seq_count, tensor_count,
 ):
-    size = q_gain.shape[1]
-    group = q_raw.shape[1] // size
-    count = seen.shape[2] // group
-    rows = v_raw.shape[1]
-    chunks = row_chunks(rows)
+    c = lax.axis_index("conv")
+    z = lax.axis_index("seq")
+    x = lax.axis_index("tensor")
+    tiles, row_local, features = k_hbm.shape
+    size = q_gain_ref.shape[1]
+    count = q_hbm.shape[0]
+    width = qa.shape[2]
+    lanes = qs.shape[1]
+    group = width // size
+    parts = seq_count * tensor_count
+    heads_side = features // size // tensor_count
     scale = 1.0 / math.sqrt(size)
-    at = pl.ds(pl.multiple_of(block * count, count), count)
-    for g in range(group):
-        raw = q_raw[at, pl.ds(g * size, size)].astype(jnp.float32)
-        normed = raw * inverse_rms(raw) * (q_gain * (scale * LOG2E))
-        qs[pl.ds(g * count, count), :] = normed.astype(jnp.bfloat16)
-        qst[:, pl.ds(g * count, count)] = normed.T.astype(jnp.bfloat16)
-    seen_row = seen[block]
+
+    def at(conv, seq, tensor):
+        return {"conv": conv, "seq": seq, "tensor": tensor}
+
+    def remote(src, dst, send, recv, device):
+        return pltpu.make_async_remote_copy(
+            src_ref=src, dst_ref=dst, send_sem=send, recv_sem=recv,
+            device_id=device, device_id_type=pl.DeviceIdType.MESH,
+        )
+
+    def steps(j):
+        return seq_count - 1 - j // tensor_count, tensor_count - 1 - j % tensor_count
+
+    def target(j):
+        k, e = steps(j)
+        return lax.rem(z + k, seq_count), lax.rem(x + e, tensor_count)
+
+    def source(j):
+        k, e = steps(j)
+        return lax.rem(z + seq_count - k, seq_count), lax.rem(x + tensor_count - e, tensor_count)
+
+    def head_lanes(seq, tensor):
+        return pl.ds(pl.multiple_of((tensor * heads_side + seq) * size, size), size)
+
+    def group_lanes(seq):
+        return pl.ds(pl.multiple_of(seq * width, width), width)
+
+    partner = c + 1 - 2 * lax.rem(c, 2)
+    siblings = [lax.rem(c + 2 * m, conv_count) for m in range(1, conv_count // 2)]
+    fars = [lax.rem(partner + 2 * m, conv_count) for m in range(1, conv_count // 2)]
+    others = [partner] + siblings
+    own = parts - 1
+
+    barrier = pltpu.get_barrier_semaphore()
+    peers = [at(c, *target(j)) for j in range(own)] + [at(other, z, x) for other in others]
+    for peer in peers:
+        pl.semaphore_signal(barrier, inc=1, device_id=peer, device_id_type=pl.DeviceIdType.MESH)
+    pl.semaphore_wait(barrier, len(peers))
+
+    token_pairs = ((q_hbm, qa), (do_hbm, da))
+    stores = (k_hbm, v_hbm)
+
+    def q_copy(part, i):
+        store, into = token_pairs[part]
+        to = lax.rem(z + seq_count - i, seq_count)
+        return remote(
+            store.at[:, group_lanes(to)], into.at[z],
+            q_send.at[part, i], q_recv.at[part, i], at(c, to, x),
+        )
+
+    def own_q_copy(part):
+        store, into = token_pairs[part]
+        return pltpu.make_async_copy(store.at[:, group_lanes(z)], into.at[z], own_q_sem.at[part])
+
+    for i in range(1, seq_count):
+        for part in range(2):
+            q_copy(part, i).start()
+
+    def raw_copy(j, part, n):
+        src = stores[part].at[:, :, head_lanes(*target(j))]
+        return remote(
+            src, raw.at[c, j, part],
+            conv_send.at[n, part, j], conv_recv.at[n, part, j], at(others[n], z, x),
+        )
+
+    def own_copy(j, part):
+        src = stores[part].at[:, :, head_lanes(*target(j))]
+        return pltpu.make_async_copy(src, raw.at[c, j, part], own_sem.at[part, j])
+
+    @pl.loop(0, parts)
+    def _(j):
+        for n in reversed(range(len(others))):
+            for part in range(2):
+                raw_copy(j, part, n).start()
+        for part in range(2):
+            own_copy(j, part).start()
+
+    for part in range(2):
+        own_q_copy(part).start()
+
+    seen_all = jnp.minimum(visible[pl.ds(c, 1), :], counts[c])
+    for b in range(seq_count):
+        piece = seen_all[:, b * count:(b + 1) * count]
+        seen[b] = jnp.concatenate([piece] * group, axis=1)
     acc[...] = jnp.zeros_like(acc)
     total[...] = jnp.zeros_like(total)
     dqt[...] = jnp.zeros_like(dqt)
-
-    for tile in range(tiles):
-        @pl.when(last_seen > tile)
-        def _(tile=tile):
-            mask = (seen_row > tile).astype(jnp.float32)
-            part = jnp.zeros(acc.shape, jnp.float32)
-            part_sum = jnp.zeros(total.shape, jnp.float32)
-            for start, length in chunks:
-                here = pl.ds(start, length)
-                w = jnp.exp2(dot(kn[tile, here, :], qst[...]))
-                if start + length > TILE:
-                    ids = start + lax.broadcasted_iota(jnp.int32, w.shape, 0)
-                    w = jnp.where(ids < TILE, w, 0.0)
+    q_gain = q_gain_ref[...]
+    k_gain = k_gain_ref[...]
+    gate_value = jnp.tanh(jnp.full((1, size), gate[0], jnp.float32))[:, :1]
+
+    def relay(ref, j, m, send, recv):
+        other = siblings[m]
+        return remote(ref.at[other, j], ref.at[other, j], send.at[m, j], recv.at[m, j], at(partner, z, x))
+
+    def relayed(ref, j, m, send, recv):
+        return remote(ref.at[fars[m], j], ref.at[fars[m], j], send.at[m, j], recv.at[m, j], at(partner, z, x))
+
+    def kv_copy(j):
+        return remote(sel.at[j], kvc.at[j], kv_send.at[j], kv_recv.at[j], at(c, *target(j)))
+
+    @pl.loop(0, parts)
+    def _(j):
+        for m, other in enumerate(siblings):
+            came = len(siblings) - m
+            for part in range(2):
+                remote(
+                    raw.at[other, j, part], raw.at[other, j, part],
+                    conv_send.at[came, part, j], conv_recv.at[came, part, j], at(other, z, x),
+                ).wait_recv()
+            relay(raw, j, m, relay_send, relay_recv).start()
+        for part in range(2):
+            own_copy(j, part).wait()
+            remote(
+                raw.at[partner, j, part], raw.at[partner, j, part],
+                conv_send.at[0, part, j], conv_recv.at[0, part, j], at(partner, z, x),
+            ).wait_recv()
+        for m in range(len(siblings)):
+            relayed(raw, j, m, relay_send, relay_recv).wait_recv()
+        for tile in range(tiles):
+            for part in range(2):
+                value = raw[0, j, part, tile]
+                for conv in range(1, conv_count):
+                    value = jnp.where(owners[tile, c] == conv, raw[conv, j, part, tile], value)
+                sel[j, part, tile] = value
+
+        @pl.when(j < own)
+        def _():
+            kv_copy(j).start()
+
+    kvc[own] = sel[own]
+
+    @pl.loop(0, seq_count)
+    def _(i):
+        block = lax.rem(z + i, seq_count)
+
+        @pl.when(i == 0)
+        def _():
+            for part in range(2):
+                own_q_copy(part).wait()
+
+        @pl.when(i > 0)
+        def _():
+            for part, (store, into) in enumerate(token_pairs):
+                remote(
+                    store.at[:, group_lanes(z)], into.at[block],
+                    q_send.at[part, i], q_recv.at[part, i], at(c, block, x),
+                ).wait_recv()
+
+        for g in range(group):
+            piece = pl.ds(g * size, size)
+            some = pl.ds(g * count, count)
+            query = qa[block, :, piece].astype(jnp.float32)
+            normed = query * inverse_rms(query) * (q_gain * (scale * LOG2E))
+            qs[block, some, :] = normed.astype(jnp.bfloat16)
+            qst[block, :, some] = normed.T.astype(jnp.bfloat16)
+            dt[block, :, some] = (da[block, :, piece].astype(jnp.float32) * gate_value).T
+
+    @pl.loop(0, parts)
+    def _(n):
+        j = lax.rem(n + parts - tensor_count, parts)
+
+        @pl.when(j < own)
+        def _():
+            kv_copy(j).wait_recv()
+
+        for tile in range(tiles):
+            key = kvc[j, 0, tile].astype(jnp.float32)
+            normed = key * inverse_rms(key) * k_gain
+            kn[j, tile] = normed.astype(jnp.bfloat16)
+            kt[j, tile] = normed.T.astype(jnp.bfloat16)
+            vt[j, tile] = kvc[j, 1, tile].astype(jnp.float32).T.astype(jnp.bfloat16)
+        from_seq, from_tensor = source(j)
+        left = TILE - (from_seq * tensor_count + from_tensor) * row_local
+
+        @pl.loop(0, seq_count)
+        def _(b):
+            seen_row = seen[b]
+            part = jnp.zeros(acc.shape[1:], jnp.float32)
+            part_sum = jnp.zeros(total.shape[1:], jnp.float32)
+            for tile in range(tiles):
+                limit = jnp.where(seen_row > tile, left, 0)
+                w = jnp.exp2(dot(kn[j, tile], qst[b]))
+                w = jnp.where(lax.broadcasted_iota(jnp.int32, w.shape, 0) < limit, w, 0.0)
                 part_sum = part_sum + jnp.sum(w, axis=0, keepdims=True)
                 w_bf = w.astype(jnp.bfloat16)
-                wts[tile, here, :] = w_bf
-                part = part + dot(vt[tile, :, here], w_bf)
-            acc[...] += part * mask
-            total[...] += part_sum * mask
-
-    safe = jnp.where(total[...] > 0, total[...], 1.0)
-    inv = 1.0 / safe
-    ctx = acc[...] * inv
-    for g in range(group):
-        lanes = pl.ds(g * count, count)
-        grad = d_out[at, pl.ds(g * size, size)].astype(jnp.float32) * gate_value
-        dost[:, lanes] = grad.T
-        att_out[at, pl.ds(g * size, size)] = (
-            (gate_value * ctx[:, g * count:(g + 1) * count]).T.astype(jnp.bfloat16)
-        )
-    scaled = (dost[...] * inv).astype(jnp.bfloat16)
-    scaled32 = scaled.astype(jnp.float32)
-    delta = jnp.sum(scaled32 * ctx, axis=0, keepdims=True)
-
-    for tile in range(tiles):
-        @pl.when(last_seen > tile)
-        def _(tile=tile):
-            mask = (seen_row > tile).astype(jnp.float32)
-            cut32 = scaled32 * mask
-            cut = cut32.astype(jnp.bfloat16)
-            for g in range(group):
-                dos[pl.ds(g * count, count), :] = (
-                    cut32[:, g * count:(g + 1) * count].T.astype(jnp.bfloat16)
-                )
-            low = delta * mask
-            part = jnp.zeros(dqt.shape, jnp.float32)
-            for start, length in chunks:
-                here = pl.ds(start, length)
-                w_bf = wts[tile, here, :]
-                dp = dot(v_raw[tile, here, :], cut)
+                wts[j, b, tile] = w_bf
+                part = part + dot(vt[j, tile], w_bf)
+            acc[b] += part
+            total[b] += part_sum
+
+    def out_copy(part, i):
+        stage, out = ((att_st, att_hbm), (dq_st, dq_hbm))[part]
+        to = lax.rem(z + i, seq_count)
+        return remote(
+            stage.at[to], out.at[:, group_lanes(z)],
+            out_send.at[part, i], out_recv.at[part, seq_count - i], at(c, to, x),
+        )
+
+    def own_out_copy(part):
+        stage, out = ((att_st, att_hbm), (dq_st, dq_hbm))[part]
+        return pltpu.make_async_copy(stage.at[z], out.at[:, group_lanes(z)], own_out_sem.at[part])
+
+    @pl.loop(0, seq_count)
+    def _(n):
+        b = lax.rem(z + n + 1, seq_count)
+        inv = 1.0 / jnp.where(total[b] > 0, total[b], 1.0)
+        ctx = acc[b] * inv
+        for g in range(group):
+            att_st[b, :, pl.ds(g * size, size)] = (
+                (gate_value * ctx[:, g * count:(g + 1) * count]).T.astype(jnp.bfloat16)
+            )
+        scaled = (dt[b] * inv).astype(jnp.bfloat16)
+        scaled32 = scaled.astype(jnp.float32)
+        scaled_t[b] = scaled
+        delta[b] = jnp.sum(scaled32 * ctx, axis=0, keepdims=True)
+
+        @pl.when(n < seq_count - 1)
+        def _():
+            out_copy(0, n + 1).start()
+
+        for g in range(group):
+            dos[b, pl.ds(g * count, count), :] = (
+                scaled32[:, g * count:(g + 1) * count].T.astype(jnp.bfloat16)
+            )
+
+    own_out_copy(0).start()
+
+    def back_copy(j, n):
+        return remote(
+            grads.at[c, j], grads.at[c, j], back_send.at[n, j], back_recv.at[n, j],
+            at(others[n], z, x),
+        )
+
+    def ret_copy(part, j):
+        out = (dk_hbm, dv_hbm)[part]
+        return remote(
+            gsel.at[j, part], out.at[:, :, head_lanes(z, x)],
+            ret_send.at[part, j], ret_recv.at[part, j], at(c, *source(j)),
+        )
+
+    def own_ret_copy(part):
+        out = (dk_hbm, dv_hbm)[part]
+        return pltpu.make_async_copy(
+            gsel.at[own, part], out.at[:, :, head_lanes(z, x)], own_ret_sem.at[part]
+        )
+
+    def pass_back(j):
+        for m, other in enumerate(siblings):
+            came = len(siblings) - m
+            remote(
+                grads.at[other, j], grads.at[other, j], back_send.at[came, j],
+                back_recv.at[came, j], at(other, z, x),
+            ).wait_recv()
+            relay(grads, j, m, backrelay_send, backrelay_recv).start()
+        remote(
+            grads.at[partner, j], grads.at[partner, j], back_send.at[0, j],
+            back_recv.at[0, j], at(partner, z, x),
+        ).wait_recv()
+        for m in range(len(siblings)):
+            relayed(grads, j, m, backrelay_send, backrelay_recv).wait_recv()
+        for tile in range(tiles):
+            for part in range(2):
+                value = jnp.zeros((row_local, size), jnp.bfloat16)
+                for conv in range(conv_count):
+                    value = jnp.where(owners[tile, conv] == c, grads[conv, j, part, tile], value)
+                gsel[j, part, tile] = value
+
+        @pl.when(j < own)
+        def _():
+            for part in range(2):
+                ret_copy(part, j).start()
+
+    @pl.loop(0, parts)
+    def _(j):
+        dk[...] = jnp.zeros_like(dk)
+        dv[...] = jnp.zeros_like(dv)
+
+        @pl.loop(0, seq_count)
+        def _(b):
+            low = delta[b]
+            part = jnp.zeros(dqt.shape[1:], jnp.float32)
+            for tile in range(tiles):
+                w_bf = wts[j, b, tile]
+                dp = dot(kvc[j, 1, tile], scaled_t[b])
                 ds = (w_bf.astype(jnp.float32) * (dp - low)).astype(jnp.bfloat16)
-                dv[tile, here, :] += dot(w_bf, dos[...])
-                dk[tile, here, :] += dot(ds, qs[...])
-                part = part + dot(kt[tile, :, here], ds)
-            dqt[...] += part
-
-    for g in range(group):
-        raw = q_raw[at, pl.ds(g * size, size)].astype(jnp.float32)
-        grad = dqt[:, pl.ds(g * count, count)].T * (q_gain * scale)
-        dq_out[at, pl.ds(g * size, size)] = norm_back(raw, inverse_rms(raw), grad).astype(
-            jnp.bfloat16
-        )
-
-
-def head_kernel(
-    last, counts, gate, q_raw, d_out, k_raw, v_raw, seen, q_gain_ref, k_gain_ref,
-    att_out, dq_out, dk_out, dv_out,
-    kn, kt, vt, wts, qs, qst, dos, dost, acc, total, dqt, dk, dv,
-):
-    tiles = k_raw.shape[0]
-    q_gain = q_gain_ref[...]
-    k_gain = k_gain_ref[...]
-    dk[...] = jnp.zeros_like(dk)
-    dv[...] = jnp.zeros_like(dv)
-    for tile in range(tiles):
-        prepare_tile(tile, k_raw, v_raw, k_gain, kn, kt, vt)
-
-    @pl.loop(0, seen.shape[0])
-    def _(block):
-        attend_block(
-            block, last[block], tiles, q_raw, d_out, seen, gate[0], q_gain, v_raw, kn, kt, vt,
-            att_out, dq_out, wts, qs, qst, dos, dost, acc, total, dqt, dk, dv,
-        )
-
-    for tile in range(tiles):
-        finish_tile(tile, k_raw, k_gain, dk, dv, dk_out, dv_out)
-
-
-def core_scratch(tiles, rows, size, lanes):
-    bf, f32 = jnp.bfloat16, jnp.float32
-    return [
-        pltpu.VMEM((tiles, rows, size), bf),
-        pltpu.VMEM((tiles, size, rows), bf),
-        pltpu.VMEM((tiles, size, rows), bf),
-        pltpu.VMEM((tiles, rows, lanes), bf),
-        pltpu.VMEM((lanes, size), bf),
-        pltpu.VMEM((size, lanes), bf),
-        pltpu.VMEM((lanes, size), bf),
-        pltpu.VMEM((size, lanes), f32),
-        pltpu.VMEM((size, lanes), f32),
-        pltpu.VMEM((1, lanes), f32),
-        pltpu.VMEM((size, lanes), f32),
-        pltpu.VMEM((tiles, rows, size), f32),
-        pltpu.VMEM((tiles, rows, size), f32),
-    ]
-
-
-def move_convs(outgoing):
-    count = len(outgoing)
-    return [outgoing[0]] + [
-        lax.ppermute(outgoing[shift], "conv", [(i, (i + shift) % count) for i in range(count)])
-        for shift in range(1, count)
-    ]
-
-
-def choose(arrived, index):
-    chosen = arrived[0]
-    for shift in range(1, len(arrived)):
-        chosen = jnp.where(index == shift, arrived[shift], chosen)
-    return chosen
+                dv[tile] += dot(w_bf, dos[b])
+                dk[tile] += dot(ds, qs[b])
+                part = part + dot(kt[j, tile], ds)
+            dqt[b] += part
+
+        for tile in range(tiles):
+            key = kvc[j, 0, tile].astype(jnp.float32)
+            grad = dk[tile] * (1.0 / LOG2E) * k_gain
+            grads[c, j, 0, tile] = norm_back(key, inverse_rms(key), grad).astype(jnp.bfloat16)
+            grads[c, j, 1, tile] = dv[tile].astype(jnp.bfloat16)
+        for n in reversed(range(len(others))):
+            back_copy(j, n).start()
+
+        @pl.when(j == parts // 2)
+        def _():
+            pass_back(0)
+
+    @pl.loop(0, seq_count)
+    def _(n):
+        b = lax.rem(z + n + 1, seq_count)
+        for g in range(group):
+            piece = pl.ds(g * size, size)
+            query = qa[b, :, piece].astype(jnp.float32)
+            grad = dqt[b, :, pl.ds(g * count, count)].T * (q_gain * scale)
+            dq_st[b, :, piece] = norm_back(query, inverse_rms(query), grad).astype(jnp.bfloat16)
+
+        @pl.when(n < seq_count - 1)
+        def _():
+            out_copy(1, n + 1).start()
+
+    own_out_copy(1).start()
+
+    @pl.loop(1, parts)
+    def _(j):
+        pass_back(j)
+
+    for part in range(2):
+        own_ret_copy(part).start()
+
+    @pl.loop(0, parts)
+    def _(j):
+        for n in range(len(others)):
+            for part in range(2):
+                raw_copy(j, part, n).wait_send()
+            back_copy(j, n).wait_send()
+        for m in range(len(siblings)):
+            relay(raw, j, m, relay_send, relay_recv).wait_send()
+            relay(grads, j, m, backrelay_send, backrelay_recv).wait_send()
+
+    @pl.loop(0, own)
+    def _(j):
+        kv_copy(j).wait_send()
+        for part in range(2):
+            ret_copy(part, j).wait_send()
+            out = (dk_hbm, dv_hbm)[part]
+            remote(
+                gsel.at[j, part], out.at[:, :, head_lanes(*target(j))],
+                ret_send.at[part, j], ret_recv.at[part, j], at(c, *target(j)),
+            ).wait_recv()
+
+    for part, (stage, out) in enumerate(((att_st, att_hbm), (dq_st, dq_hbm))):
+        for i in range(1, seq_count):
+            q_copy(part, i).wait_send()
+            came = lax.rem(z + seq_count - i, seq_count)
+            remote(
+                stage.at[came], out.at[:, group_lanes(lax.rem(z + i, seq_count))],
+                out_send.at[part, i], out_recv.at[part, i], at(c, came, x),
+            ).wait()
+        own_out_copy(part).wait()
+        own_ret_copy(part).wait()
 
 
 def head_shards(queries, keys, values, q_gain, k_gain, gate, tile_count, tile_owner, visible, d_out):
     conv_count = lax.axis_size("conv")
     tensor_count = lax.axis_size("tensor")
     seq_count = lax.axis_size("seq")
-    conv_index = lax.axis_index("conv")
-    slot_count, row_local, features = keys.shape
+    tiles, row_local, features = keys.shape
     size = q_gain.shape[0]
-    block_tokens, width = queries.shape[1:]
-    group = width // (features // tensor_count)
-    lanes = group * block_tokens
-    everyone = ("conv", "seq", "tensor")
-
-    own_owners = lax.dynamic_index_in_dim(tile_owner, conv_index, 0, keepdims=False)
-    own_count = lax.dynamic_index_in_dim(tile_count, conv_index, 0, keepdims=False)
-    seen = jnp.minimum(lax.dynamic_index_in_dim(visible, conv_index, 0, keepdims=False), own_count)
-    seen = seen.reshape(seq_count, 1, block_tokens)
-    last = seen[:, 0, -1]
-    seen = jnp.tile(seen, (1, 1, group))
-
-    both = jnp.stack([queries[0], d_out[0]]).reshape(2, block_tokens, seq_count, width // seq_count)
-    both = lax.all_to_all(both, "seq", split_axis=2, concat_axis=1, tiled=True)
-    both = both.reshape(2, seq_count * block_tokens, width // seq_count)
-
-    goes = tile_owner == conv_index
-    slot_of = jnp.argmax(goes, axis=1)
-    shifts = list(range(conv_count))
-    own_shift = jnp.remainder(conv_index - own_owners, conv_count)
-
-    def fetch(stored):
-        outgoing = [
-            lax.dynamic_index_in_dim(
-                stored, slot_of[jnp.remainder(conv_index + shift, conv_count)], 0, keepdims=False
-            )
-            for shift in shifts
-        ]
-        arrived = move_convs(outgoing)
-        mine = jnp.stack([choose(arrived, own_shift[tile]) for tile in range(slot_count)])
-        mine = mine.reshape(slot_count, row_local, tensor_count, seq_count, size)
-        mine = jnp.transpose(mine, (3, 2, 0, 1, 4)).reshape(-1, slot_count, row_local, size)
-        mine = lax.all_to_all(mine, ("seq", "tensor"), split_axis=0, concat_axis=0, tiled=True)
-        return jnp.transpose(mine, (1, 0, 2, 3)).reshape(slot_count, -1, size)
-
-    key_tiles = fetch(keys)
-    value_tiles = fetch(values)
-    rows = key_tiles.shape[1]
+    count, width_all = queries.shape[1:]
+    width = width_all // seq_count
+    lanes = width // size * count
+    bf, f32 = jnp.bfloat16, jnp.float32
+    parts = seq_count * tensor_count
+    far = conv_count // 2 - 1
+    chunk = (2, tiles, row_local, size)
+    v, dma = pltpu.VMEM, pltpu.SemaphoreType.DMA
 
     vmem = pl.BlockSpec(memory_space=pltpu.VMEM)
     smem = pl.BlockSpec(memory_space=pltpu.SMEM)
+    hbm = pl.BlockSpec(memory_space=pl.ANY)
     att, dq, dk, dv = pl.pallas_call(
-        head_kernel,
-        out_shape=[jax.ShapeDtypeStruct(both.shape[1:], jnp.bfloat16)] * 2
-        + [jax.ShapeDtypeStruct((slot_count, rows, size), jnp.bfloat16)] * 2,
-        in_specs=[smem] * 3 + [vmem] * 7,
-        out_specs=[vmem] * 4,
-        scratch_shapes=core_scratch(slot_count, rows, size, lanes),
-        compiler_params=pltpu.CompilerParams(vmem_limit_bytes=60 << 20),
+        partial(
+            head_kernel, conv_count=conv_count, seq_count=seq_count, tensor_count=tensor_count
+        ),
+        out_shape=[jax.ShapeDtypeStruct((count, width_all), bf)] * 2
+        + [jax.ShapeDtypeStruct(keys.shape, bf)] * 2,
+        in_specs=[smem] * 3 + [vmem] * 3 + [hbm] * 4,
+        out_specs=[hbm] * 4,
+        scratch_shapes=[
+            v((conv_count, parts) + chunk, bf),
+            v((parts,) + chunk, bf),
+            v((parts,) + chunk, bf),
+            v((seq_count, count, width), bf),
+            v((seq_count, count, width), bf),
+            v((seq_count, 1, lanes), jnp.int32),
+            v((parts, tiles, row_local, size), bf),
+            v((parts, tiles, size, row_local), bf),
+            v((parts, tiles, size, row_local), bf),
+            v((parts, seq_count, tiles, row_local, lanes), bf),
+            v((seq_count, lanes, size), bf),
+            v((seq_count, size, lanes), bf),
+            v((seq_count, size, lanes), f32),
+            v((seq_count, size, lanes), f32),
+            v((seq_count, 1, lanes), f32),
+            v((seq_count, size, lanes), bf),
+            v((seq_count, lanes, size), bf),
+            v((seq_count, 1, lanes), f32),
+            v((seq_count, size, lanes), f32),
+            v((tiles, row_local, size), f32),
+            v((tiles, row_local, size), f32),
+            v((seq_count, count, width), bf),
+            v((seq_count, count, width), bf),
+            v((conv_count, parts) + chunk, bf),
+            v((parts,) + chunk, bf),
+            dma((2, parts)), dma((far + 1, 2, parts)), dma((far + 1, 2, parts)),
+            dma((far, parts)), dma((far, parts)), dma((parts,)), dma((parts,)),
+            dma((2, seq_count)), dma((2, seq_count)), dma((2,)),
+            dma((2, seq_count)), dma((2, seq_count)), dma((2,)),
+            dma((far + 1, parts)), dma((far + 1, parts)), dma((far, parts)), dma((far, parts)),
+            dma((2, parts)), dma((2, parts)), dma((2,)),
+        ],
+        compiler_params=pltpu.CompilerParams(
+            collective_id=0, has_side_effects=True, vmem_limit_bytes=60 << 20
+        ),
     )(
-        last, own_count.reshape(1), jnp.tanh(gate), both[0], both[1], key_tiles, value_tiles,
-        seen, q_gain[None], k_gain[None],
-    )
-
-    tile_of = jnp.argmax(own_owners[None, :] == jnp.arange(conv_count)[:, None], axis=1)
-    taker = jnp.argmax(goes, axis=0)
-    used = jnp.any(goes, axis=0)
-    taker_shift = jnp.remainder(conv_index - taker, conv_count)
-
-    def give_back(grads):
-        grads = jnp.transpose(grads.reshape(slot_count, -1, row_local, size), (1, 0, 2, 3))
-        grads = lax.all_to_all(grads, ("seq", "tensor"), split_axis=0, concat_axis=0, tiled=True)
-        grads = grads.reshape(seq_count, tensor_count, slot_count, row_local, size)
-        grads = jnp.transpose(grads, (2, 3, 1, 0, 4)).reshape(slot_count, row_local, features)
-        outgoing = [
-            lax.dynamic_index_in_dim(
-                grads, tile_of[jnp.remainder(conv_index + shift, conv_count)], 0, keepdims=False
-            )
-            for shift in shifts
-        ]
-        arrived = move_convs(outgoing)
-        zero = jnp.zeros((), jnp.bfloat16)
-        return jnp.stack(
-            [
-                jnp.where(used[slot], choose(arrived, taker_shift[slot]), zero)
-                for slot in range(slot_count)
-            ]
-        )
-
-    d_keys = give_back(dk)
-    outs = jnp.stack([att, dq])
-    outs, d_keys = lax.optimization_barrier((outs, d_keys))
-    outs = outs.reshape(2, seq_count, block_tokens, width // seq_count)
-    outs = lax.all_to_all(outs, "seq", split_axis=1, concat_axis=3, tiled=True)
-    attended = outs[0].reshape(1, block_tokens, width)
-    d_queries = outs[1].reshape(1, block_tokens, width)
-
-    return (attended, d_queries, d_keys, give_back(dv))
+        tile_owner.T, tile_count, gate, visible, q_gain[None], k_gain[None],
+        queries[0], d_out[0], keys, values,
+    )
+    return (att[None], dq[None], dk, dv)
 
 
 def shards(queries, keys, *rest):
     heads = keys.shape[2] // rest[1].shape[0]
-    split = lax.axis_size("seq") * lax.axis_size("tensor")
-    return (head_shards if heads == split else row_shards)(queries, keys, *rest)
+    seq_count, tensor_count = lax.axis_size("seq"), lax.axis_size("tensor")
+    conv_count = lax.axis_size("conv")
+    fits = heads == seq_count * tensor_count and conv_count % 2 == 0 and conv_count > 2
+    fits = fits and keys.shape[1] % 16 == 0
+    return (head_shards if fits else row_shards)(queries, keys, *rest)
 
 
 def solution(mesh):

time: 224 us -> 147 us (0.66)
  Pallas kernels: 20.6 us -> 139 us
  waiting for transfers between devices: 84.2 us -> 0 us
  starting transfers between devices: 51.8 us -> 0 us
  between operations: 24.4 us -> 1.31 us
  local copies, waits for them, and re-layouts: 26.3 us -> 5.15 us
  other arithmetic: 13 us -> 0 us
    pallas_call x1, Pallas kernels: 20.6 us -> 139 us  [head_shards(): pl.pallas_call(partial(head_kernel, conv_count=conv_count, seq_count=seq_...]
    ppermute x12 -> x0, waiting for transfers between devices: 53.4 us -> none  [move_convs(): lax.ppermute(outgoing[shift], 'conv', [(i, (i + shift) % count) for i in...]
    all_to_all x6 -> x0, starting transfers between devices: 32.9 us -> none  [the longest x2 12.3 us: give_back(): lax.all_to_all(grads, ('seq', 'tensor'), split_axis=0, concat_axis=0, til...]
    all_to_all x6 -> x0, waiting for transfers between devices: 30.8 us -> none  [the longest x2 17.7 us: give_back(): lax.all_to_all(grads, ('seq', 'tensor'), split_axis=0, concat_axis=0, til...]
    ppermute x12 -> x0, starting transfers between devices: 18.9 us -> none  [move_convs(): lax.ppermute(outgoing[shift], 'conv', [(i, (i + shift) % count) for i in...]
    another operation x10 -> x0, other arithmetic: 8.88 us -> none  [the longest x4 5.94 us: give_back(): jnp.stack([jnp.where(used[slot], choose(arrived, taker_shift[slot]), zero...]
    reshape x8 -> x0, local copies, waits for them, and re-layouts: 8.06 us -> none  [the longest x2 3.1 us: give_back(): grads.reshape(slot_count, -1, row_local, size)]
    slice x6 -> x0, local copies, waits for them, and re-layouts: 3.09 us -> none  [the longest x1 1.03 us: head_shards(): both[1]]
  transfers between devices with their start and end apart: 18 -> 0, of which waited for: 13 -> 0; matrix products, arithmetic and copies ran while one was open for 13% -> 0% of each run, Pallas kernels for 0% -> 0%
where the time goes in v2:
time: 147 us; the launch traced here: 146 us
  Pallas kernels  139 us (95%)
  local copies, waits for them, and re-layouts  5.15 us (4%)
    pallas_call x1, Pallas kernels, head_shards(): pl.pallas_call(partial(head_kernel, conv_count=conv_count, seq_count=seq_...  139 us
    unnamed x10, local copies, waits for them, and re-layouts  5.15 us

profile of v2, /device:TPU:9, one launch (start us, length us, event | category | flops | bytes accessed | tf_op | source)
XLA Modules:
  0.0 145.5 jit_solution(3739762084602950250)
XLA Ops:
  1.3 139.0 %shard_map.129 = (bf16[128,2048]{1,0:T(8,128)(2,1)}, bf16[128,2048]{1,0:T(8,128)(2,1)}, bf16[2,208,1024]{2,1,0:T(8,128)(2,1)}, bf16[2,208,1024]{2,1,0:T(8,128)(2,1)}) custom-call(s32[2,4]{1,0:T(2,128)} %bitcast.11, s32[4]{0:T(128)} %counts.1, f32[1]{0:T(128)S(6)} %copy.18.gate, s32[4,512]{1,0:T(4,128)} %visible.1, f32[1,128]{1,0:T(1,128)} %bitcast.12, ...), custom_call_target="tpu_custom_call" | custom-call | tf_op jit(solution)/shard_map/pallas_call | solution.py:705
  140.3 0.0 copy-start.2
  140.3 0.0 copy-start.1
  140.4 2.0 %copy.19 = bf16[1,128,2048]{2,1,0:T(8,128)(2,1)} copy(bf16[1,128,2048]{2,1,0:T(8,128)(2,1)} %bitcast.8) | data formatting | bytes 1048576
  142.3 0.0 copy-done.2
  142.3 0.8 copy.20
  143.1 0.0 copy-done.1
  143.1 0.0 copy-start
  143.1 0.9 copy.21
  144.0 0.6 copy-done
  144.6 0.9 copy.22
Async XLA Ops:
  140.3 2.0 %copy-start.2 = (bf16[128,2048]{1,0:T(8,128)(2,1)S(1)}, bf16[128,2048]{1,0:T(8,128)(2,1)}, u32[]{:S(2)}) copy-start(bf16[128,2048]{1,0:T(8,128)(2,1)} %get-tuple-element.9) | copy-start | bytes 1572868
  140.3 2.8 %copy-start.1 = (bf16[2,208,1024]{2,1,0:T(8,128)(2,1)S(1)}, bf16[2,208,1024]{2,1,0:T(8,128)(2,1)}, u32[]{:S(2)}) copy-start(bf16[2,208,1024]{2,1,0:T(8,128)(2,1)} %get-tuple-element.18) | copy-start | bytes 2555908
  143.1 1.5 %copy-start = (bf16[2,208,1024]{2,1,0:T(8,128)(2,1)S(1)}, bf16[2,208,1024]{2,1,0:T(8,128)(2,1)}, u32[]{:S(2)}) copy-start(bf16[2,208,1024]{2,1,0:T(8,128)(2,1)} %get-tuple-element.19) | copy-start | bytes 2555908

commit v3 on v2

--- a/solution.py
+++ b/solution.py
@@ -308,7 +308,7 @@
     owners, counts, gate, visible, q_gain_ref, k_gain_ref, q_hbm, do_hbm, k_hbm, v_hbm,
     att_hbm, dq_hbm, dk_hbm, dv_hbm,
     raw, sel, kvc, qa, da, seen, kn, kt, vt, wts, qs, qst, dt, acc, total, scaled_t, dos, delta,
-    dqt, dk, dv, att_st, dq_st, grads, gsel,
+    dqt, dss, att_st, dq_st, grads, gsel,
     own_sem, conv_send, conv_recv, relay_send, relay_recv, kv_send, kv_recv,
     q_send, q_recv, own_q_sem, out_send, out_recv, own_out_sem,
     back_send, back_recv, backrelay_send, backrelay_recv, ret_send, ret_recv, own_ret_sem,
@@ -321,9 +321,10 @@
     size = q_gain_ref.shape[1]
     count = q_hbm.shape[0]
     width = qa.shape[2]
-    lanes = qs.shape[1]
     group = width // size
+    lanes = group * count
     parts = seq_count * tensor_count
+    rows = tiles * row_local
     heads_side = features // size // tensor_count
     scale = 1.0 / math.sqrt(size)
 
@@ -339,6 +340,23 @@
     def steps(j):
         return seq_count - 1 - j // tensor_count, tensor_count - 1 - j % tensor_count
 
+    half = z // (seq_count // 2)
+
+    def hop(q):
+        k = 1 + (q + seq_count // 2 + seq_count - 3) % (seq_count - 1)
+        k = (q + seq_count - 1) // seq_count * k
+        return lax.rem(k + half * (seq_count - 2 * k), seq_count)
+
+    def place(k, n):
+        return (seq_count - 1 - k) * tensor_count + n % tensor_count
+
+    def send_order(n):
+        return place(hop(n // tensor_count), n)
+
+    def back_order(n):
+        n = lax.rem(n + tensor_count, parts)
+        return place(lax.rem(seq_count - hop(n // tensor_count), seq_count), n)
+
     def target(j):
         k, e = steps(j)
         return lax.rem(z + k, seq_count), lax.rem(x + e, tensor_count)
@@ -349,6 +367,9 @@
 
     def head_lanes(seq, tensor):
         return pl.ds(pl.multiple_of((tensor * heads_side + seq) * size, size), size)
+
+    def block_lanes(b, start=0, length=lanes):
+        return pl.ds(pl.multiple_of(b * lanes + start, size), length)
 
     def group_lanes(seq):
         return pl.ds(pl.multiple_of(seq * width, width), width)
@@ -380,9 +401,10 @@
         store, into = token_pairs[part]
         return pltpu.make_async_copy(store.at[:, group_lanes(z)], into.at[z], own_q_sem.at[part])
 
-    for i in range(1, seq_count):
+    @pl.loop(1, seq_count)
+    def _(q):
         for part in range(2):
-            q_copy(part, i).start()
+            q_copy(part, seq_count - hop(q)).start()
 
     def raw_copy(j, part, n):
         src = stores[part].at[:, :, head_lanes(*target(j))]
@@ -396,7 +418,8 @@
         return pltpu.make_async_copy(src, raw.at[c, j, part], own_sem.at[part, j])
 
     @pl.loop(0, parts)
-    def _(j):
+    def _(step):
+        j = send_order(step)
         for n in reversed(range(len(others))):
             for part in range(2):
                 raw_copy(j, part, n).start()
@@ -427,8 +450,35 @@
     def kv_copy(j):
         return remote(sel.at[j], kvc.at[j], kv_send.at[j], kv_recv.at[j], at(c, *target(j)))
 
+    def take_tokens(q):
+        i = lax.rem(seq_count - hop(q), seq_count)
+        block = lax.rem(z + i, seq_count)
+
+        @pl.when(q == 0)
+        def _():
+            for part in range(2):
+                own_q_copy(part).wait()
+
+        @pl.when(q > 0)
+        def _():
+            for part, (store, into) in enumerate(token_pairs):
+                remote(
+                    store.at[:, group_lanes(z)], into.at[block],
+                    q_send.at[part, i], q_recv.at[part, i], at(c, block, x),
+                ).wait_recv()
+
+        for g in range(group):
+            piece = pl.ds(g * size, size)
+            some = block_lanes(block, g * count, count)
+            query = qa[block, :, piece].astype(jnp.float32)
+            normed = query * inverse_rms(query) * (q_gain * (scale * LOG2E))
+            qs[some, :] = normed.astype(jnp.bfloat16)
+            qst[:, some] = normed.T.astype(jnp.bfloat16)
+            dt[:, some] = (da[block, :, piece].astype(jnp.float32) * gate_value).T
+
     @pl.loop(0, parts)
-    def _(j):
+    def _(step):
+        j = send_order(step)
         for m, other in enumerate(siblings):
             came = len(siblings) - m
             for part in range(2):
@@ -456,66 +506,43 @@
         def _():
             kv_copy(j).start()
 
+        @pl.when(step >= parts - seq_count)
+        def _():
+            take_tokens(step - (parts - seq_count))
+
     kvc[own] = sel[own]
-
-    @pl.loop(0, seq_count)
-    def _(i):
-        block = lax.rem(z + i, seq_count)
-
-        @pl.when(i == 0)
-        def _():
-            for part in range(2):
-                own_q_copy(part).wait()
-
-        @pl.when(i > 0)
-        def _():
-            for part, (store, into) in enumerate(token_pairs):
-                remote(
-                    store.at[:, group_lanes(z)], into.at[block],
-                    q_send.at[part, i], q_recv.at[part, i], at(c, block, x),
-                ).wait_recv()
-
-        for g in range(group):
-            piece = pl.ds(g * size, size)
-            some = pl.ds(g * count, count)
-            query = qa[block, :, piece].astype(jnp.float32)
-            normed = query * inverse_rms(query) * (q_gain * (scale * LOG2E))
-            qs[block, some, :] = normed.astype(jnp.bfloat16)
-            qst[block, :, some] = normed.T.astype(jnp.bfloat16)
-            dt[block, :, some] = (da[block, :, piece].astype(jnp.float32) * gate_value).T
 
     @pl.loop(0, parts)
     def _(n):
-        j = lax.rem(n + parts - tensor_count, parts)
+        j = send_order(n)
 
         @pl.when(j < own)
         def _():
             kv_copy(j).wait_recv()
 
-        for tile in range(tiles):
-            key = kvc[j, 0, tile].astype(jnp.float32)
-            normed = key * inverse_rms(key) * k_gain
-            kn[j, tile] = normed.astype(jnp.bfloat16)
-            kt[j, tile] = normed.T.astype(jnp.bfloat16)
-            vt[j, tile] = kvc[j, 1, tile].astype(jnp.float32).T.astype(jnp.bfloat16)
+        key = kvc[j, 0].reshape(rows, size).astype(jnp.float32)
+        normed = key * inverse_rms(key) * k_gain
+        kn[j] = normed.astype(jnp.bfloat16)
+        kt[j] = normed.T.astype(jnp.bfloat16)
+        vt[j] = kvc[j, 1].reshape(rows, size).astype(jnp.float32).T.astype(jnp.bfloat16)
         from_seq, from_tensor = source(j)
         left = TILE - (from_seq * tensor_count + from_tensor) * row_local
 
-        @pl.loop(0, seq_count)
-        def _(b):
+        for b in range(seq_count):
+            some = pl.ds(b * lanes, lanes)
             seen_row = seen[b]
-            part = jnp.zeros(acc.shape[1:], jnp.float32)
-            part_sum = jnp.zeros(total.shape[1:], jnp.float32)
+            scores = dot(kn[j], qst[:, some])
+            part_sum = jnp.zeros((1, lanes), jnp.float32)
             for tile in range(tiles):
                 limit = jnp.where(seen_row > tile, left, 0)
-                w = jnp.exp2(dot(kn[j, tile], qst[b]))
+                w = jnp.exp2(scores[tile * row_local:(tile + 1) * row_local])
                 w = jnp.where(lax.broadcasted_iota(jnp.int32, w.shape, 0) < limit, w, 0.0)
                 part_sum = part_sum + jnp.sum(w, axis=0, keepdims=True)
-                w_bf = w.astype(jnp.bfloat16)
-                wts[j, b, tile] = w_bf
-                part = part + dot(vt[j, tile], w_bf)
-            acc[b] += part
-            total[b] += part_sum
+                wts[j, pl.ds(tile * row_local, row_local), some] = w.astype(jnp.bfloat16)
+            total[:, some] += part_sum
+        for b in range(seq_count):
+            some = pl.ds(b * lanes, lanes)
+            acc[:, some] += dot(vt[j], wts[j, :, some])
 
     def out_copy(part, i):
         stage, out = ((att_st, att_hbm), (dq_st, dq_hbm))[part]
@@ -531,24 +558,27 @@
 
     @pl.loop(0, seq_count)
     def _(n):
-        b = lax.rem(z + n + 1, seq_count)
-        inv = 1.0 / jnp.where(total[b] > 0, total[b], 1.0)
-        ctx = acc[b] * inv
+        i = hop(lax.rem(n + 1, seq_count))
+        b = lax.rem(z + i, seq_count)
+        some = block_lanes(b)
+        sums = total[:, some]
+        inv = 1.0 / jnp.where(sums > 0, sums, 1.0)
+        ctx = acc[:, some] * inv
         for g in range(group):
             att_st[b, :, pl.ds(g * size, size)] = (
                 (gate_value * ctx[:, g * count:(g + 1) * count]).T.astype(jnp.bfloat16)
             )
-        scaled = (dt[b] * inv).astype(jnp.bfloat16)
+        scaled = (dt[:, some] * inv).astype(jnp.bfloat16)
         scaled32 = scaled.astype(jnp.float32)
-        scaled_t[b] = scaled
-        delta[b] = jnp.sum(scaled32 * ctx, axis=0, keepdims=True)
+        scaled_t[:, some] = scaled
+        delta[:, some] = jnp.sum(scaled32 * ctx, axis=0, keepdims=True)
 
         @pl.when(n < seq_count - 1)
         def _():
-            out_copy(0, n + 1).start()
+            out_copy(0, i).start()
 
         for g in range(group):
-            dos[b, pl.ds(g * count, count), :] = (
+            dos[block_lanes(b, g * count, count), :] = (
                 scaled32[:, g * count:(g + 1) * count].T.astype(jnp.bfloat16)
             )
 
@@ -573,7 +603,8 @@
             gsel.at[own, part], out.at[:, :, head_lanes(z, x)], own_ret_sem.at[part]
         )
 
-    def pass_back(j):
+    def pass_back(n):
+        j = back_order(n)
         for m, other in enumerate(siblings):
             came = len(siblings) - m
             remote(
@@ -600,53 +631,56 @@
                 ret_copy(part, j).start()
 
     @pl.loop(0, parts)
-    def _(j):
-        dk[...] = jnp.zeros_like(dk)
-        dv[...] = jnp.zeros_like(dv)
-
-        @pl.loop(0, seq_count)
-        def _(b):
-            low = delta[b]
-            part = jnp.zeros(dqt.shape[1:], jnp.float32)
-            for tile in range(tiles):
-                w_bf = wts[j, b, tile]
-                dp = dot(kvc[j, 1, tile], scaled_t[b])
-                ds = (w_bf.astype(jnp.float32) * (dp - low)).astype(jnp.bfloat16)
-                dv[tile] += dot(w_bf, dos[b])
-                dk[tile] += dot(ds, qs[b])
-                part = part + dot(kt[j, tile], ds)
-            dqt[b] += part
-
-        for tile in range(tiles):
-            key = kvc[j, 0, tile].astype(jnp.float32)
-            grad = dk[tile] * (1.0 / LOG2E) * k_gain
-            grads[c, j, 0, tile] = norm_back(key, inverse_rms(key), grad).astype(jnp.bfloat16)
-            grads[c, j, 1, tile] = dv[tile].astype(jnp.bfloat16)
-        for n in reversed(range(len(others))):
-            back_copy(j, n).start()
-
-        @pl.when(j == parts // 2)
+    def _(n):
+        j = back_order(n)
+        value = kvc[j, 1].reshape(rows, size)
+        for b in range(seq_count):
+            some = pl.ds(b * lanes, lanes)
+            dp = dot(value, scaled_t[:, some])
+            score = wts[j, :, some].astype(jnp.float32) * (dp - delta[:, some])
+            dss[:, some] = score.astype(jnp.bfloat16)
+        dv = dot(wts[j], dos[...])
+        dk = dot(dss[...], qs[...])
+        for b in range(seq_count):
+            some = pl.ds(b * lanes, lanes)
+            dqt[:, some] += dot(kt[j], dss[:, some])
+
+        key = kvc[j, 0].reshape(rows, size).astype(jnp.float32)
+        grad = dk * (1.0 / LOG2E) * k_gain
+        grad = norm_back(key, inverse_rms(key), grad).astype(jnp.bfloat16)
+        grads[c, j, 0] = grad.reshape(tiles, row_local, size)
+        grads[c, j, 1] = dv.astype(jnp.bfloat16).reshape(tiles, row_local, size)
+        for m in reversed(range(len(others))):
+            back_copy(j, m).start()
+
+        late = n - parts // 2
+
+        @pl.when((late >= 0) & (late % 2 == 0))
         def _():
-            pass_back(0)
+            pass_back(late // 2)
+
+    passed = (parts - parts // 2 + 1) // 2
+    pass_back(passed)
 
     @pl.loop(0, seq_count)
     def _(n):
-        b = lax.rem(z + n + 1, seq_count)
+        i = hop(lax.rem(n + 1, seq_count))
+        b = lax.rem(z + i, seq_count)
         for g in range(group):
             piece = pl.ds(g * size, size)
             query = qa[b, :, piece].astype(jnp.float32)
-            grad = dqt[b, :, pl.ds(g * count, count)].T * (q_gain * scale)
+            grad = dqt[:, block_lanes(b, g * count, count)].T * (q_gain * scale)
             dq_st[b, :, piece] = norm_back(query, inverse_rms(query), grad).astype(jnp.bfloat16)
 
         @pl.when(n < seq_count - 1)
         def _():
-            out_copy(1, n + 1).start()
+            out_copy(1, i).start()
 
     own_out_copy(1).start()
 
-    @pl.loop(1, parts)
-    def _(j):
-        pass_back(j)
+    @pl.loop(passed + 1, parts)
+    def _(n):
+        pass_back(n)
 
     for part in range(2):
         own_ret_copy(part).start()
@@ -692,11 +726,12 @@
     size = q_gain.shape[0]
     count, width_all = queries.shape[1:]
     width = width_all // seq_count
-    lanes = width // size * count
+    lanes = width_all // size * count
     bf, f32 = jnp.bfloat16, jnp.float32
     parts = seq_count * tensor_count
     far = conv_count // 2 - 1
     chunk = (2, tiles, row_local, size)
+    rows = tiles * row_local
     v, dma = pltpu.VMEM, pltpu.SemaphoreType.DMA
 
     vmem = pl.BlockSpec(memory_space=pltpu.VMEM)
@@ -716,22 +751,21 @@
             v((parts,) + chunk, bf),
             v((seq_count, count, width), bf),
             v((seq_count, count, width), bf),
-            v((seq_count, 1, lanes), jnp.int32),
-            v((parts, tiles, row_local, size), bf),
-            v((parts, tiles, size, row_local), bf),
-            v((parts, tiles, size, row_local), bf),
-            v((parts, seq_count, tiles, row_local, lanes), bf),
-            v((seq_count, lanes, size), bf),
-            v((seq_count, size, lanes), bf),
-            v((seq_count, size, lanes), f32),
-            v((seq_count, size, lanes), f32),
-            v((seq_count, 1, lanes), f32),
-            v((seq_count, size, lanes), bf),
-            v((seq_count, lanes, size), bf),
-            v((seq_count, 1, lanes), f32),
-            v((seq_count, size, lanes), f32),
-            v((tiles, row_local, size), f32),
-            v((tiles, row_local, size), f32),
+            v((seq_count, 1, lanes // seq_count), jnp.int32),
+            v((parts, rows, size), bf),
+            v((parts, size, rows), bf),
+            v((parts, size, rows), bf),
+            v((parts, rows, lanes), bf),
+            v((lanes, size), bf),
+            v((size, lanes), bf),
+            v((size, lanes), f32),
+            v((size, lanes), f32),
+            v((1, lanes), f32),
+            v((size, lanes), bf),
+            v((lanes, size), bf),
+            v((1, lanes), f32),
+            v((size, lanes), f32),
+            v((rows, lanes), bf),
             v((seq_count, count, width), bf),
             v((seq_count, count, width), bf),
             v((conv_count, parts) + chunk, bf),

time: 147 us -> 136 us (0.925)
  Pallas kernels: 139 us -> 129 us
    pallas_call x1, Pallas kernels: 139 us -> 129 us  [head_shards(): pl.pallas_call(partial(head_kernel, conv_count=conv_count, seq_count=seq_...]
where the time goes in v3:
time: 136 us; the launch traced here: 135 us
  Pallas kernels  129 us (95%)
  local copies, waits for them, and re-layouts  5.15 us (4%)
    pallas_call x1, Pallas kernels, head_shards(): pl.pallas_call(partial(head_kernel, conv_count=conv_count, seq_count=seq_...  129 us
    unnamed x10, local copies, waits for them, and re-layouts  5.15 us

profile of v3, /device:TPU:9, one launch (start us, length us, event | category | flops | bytes accessed | tf_op | source)
XLA Modules:
  0.0 135.3 jit_solution(2765604822555937171)
XLA Ops:
  1.3 128.8 %shard_map.129 = (bf16[128,2048]{1,0:T(8,128)(2,1)}, bf16[128,2048]{1,0:T(8,128)(2,1)}, bf16[2,208,1024]{2,1,0:T(8,128)(2,1)}, bf16[2,208,1024]{2,1,0:T(8,128)(2,1)}) custom-call(s32[2,4]{1,0:T(2,128)} %bitcast.11, s32[4]{0:T(128)} %counts.1, f32[1]{0:T(128)S(6)} %copy.18.gate, s32[4,512]{1,0:T(4,128)} %visible.1, f32[1,128]{1,0:T(1,128)} %bitcast.12, ...), custom_call_target="tpu_custom_call" | custom-call | tf_op jit(solution)/shard_map/pallas_call | solution.py:740
  130.1 0.0 copy-start.2
  130.1 0.0 copy-start.1
  130.1 2.0 %copy.19 = bf16[1,128,2048]{2,1,0:T(8,128)(2,1)} copy(bf16[1,128,2048]{2,1,0:T(8,128)(2,1)} %bitcast.8) | data formatting | bytes 1048576
  132.1 0.0 copy-done.2
  132.1 0.8 copy.20
  132.9 0.0 copy-done.1
  132.9 0.0 copy-start
  132.9 0.9 copy.21
  133.8 0.6 copy-done
  134.4 0.9 copy.22
Async XLA Ops:
  130.1 2.0 %copy-start.2 = (bf16[128,2048]{1,0:T(8,128)(2,1)S(1)}, bf16[128,2048]{1,0:T(8,128)(2,1)}, u32[]{:S(2)}) copy-start(bf16[128,2048]{1,0:T(8,128)(2,1)} %get-tuple-element.9) | copy-start | bytes 1572868
  130.1 2.8 %copy-start.1 = (bf16[2,208,1024]{2,1,0:T(8,128)(2,1)S(1)}, bf16[2,208,1024]{2,1,0:T(8,128)(2,1)}, u32[]{:S(2)}) copy-start(bf16[2,208,1024]{2,1,0:T(8,128)(2,1)} %get-tuple-element.18) | copy-start | bytes 2555908
  132.9 1.5 %copy-start = (bf16[2,208,1024]{2,1,0:T(8,128)(2,1)S(1)}, bf16[2,208,1024]{2,1,0:T(8,128)(2,1)}, u32[]{:S(2)}) copy-start(bf16[2,208,1024]{2,1,0:T(8,128)(2,1)} %get-tuple-element.19) | copy-start | bytes 2555908

commit v4 on v3

--- a/solution.py
+++ b/solution.py
@@ -305,9 +305,9 @@
 
 
 def head_kernel(
-    owners, counts, gate, visible, q_gain_ref, k_gain_ref, q_hbm, do_hbm, k_hbm, v_hbm,
+    owners, counts, gate, visible_hbm, q_gain_hbm, k_gain_hbm, q_hbm, do_hbm, k_hbm, v_hbm,
     att_hbm, dq_hbm, dk_hbm, dv_hbm,
-    raw, sel, kvc, qa, da, seen, kn, kt, vt, wts, qs, qst, dt, acc, total, scaled_t, dos, delta,
+    visible, q_gain_ref, k_gain_ref, small_sem, raw, sel, kvc, qa, da, seen, kn, kt, vt, wts, qs, qst, dt, acc, total, scaled_t, dos, delta,
     dqt, dss, att_st, dq_st, grads, gsel,
     own_sem, conv_send, conv_recv, relay_send, relay_recv, kv_send, kv_recv,
     q_send, q_recv, own_q_sem, out_send, out_recv, own_out_sem,
@@ -428,6 +428,16 @@
 
     for part in range(2):
         own_q_copy(part).start()
+    small = [
+        pltpu.make_async_copy(src, dst, small_sem.at[n])
+        for n, (src, dst) in enumerate(
+            ((visible_hbm, visible), (q_gain_hbm, q_gain_ref), (k_gain_hbm, k_gain_ref))
+        )
+    ]
+    for copy in small:
+        copy.start()
+    for copy in small:
+        copy.wait()
 
     seen_all = jnp.minimum(visible[pl.ds(c, 1), :], counts[c])
     for b in range(seq_count):
@@ -734,7 +744,6 @@
     rows = tiles * row_local
     v, dma = pltpu.VMEM, pltpu.SemaphoreType.DMA
 
-    vmem = pl.BlockSpec(memory_space=pltpu.VMEM)
     smem = pl.BlockSpec(memory_space=pltpu.SMEM)
     hbm = pl.BlockSpec(memory_space=pl.ANY)
     att, dq, dk, dv = pl.pallas_call(
@@ -743,9 +752,13 @@
         ),
         out_shape=[jax.ShapeDtypeStruct((count, width_all), bf)] * 2
         + [jax.ShapeDtypeStruct(keys.shape, bf)] * 2,
-        in_specs=[smem] * 3 + [vmem] * 3 + [hbm] * 4,
+        in_specs=[smem] * 3 + [hbm] * 7,
         out_specs=[hbm] * 4,
         scratch_shapes=[
+            v(visible.shape, jnp.int32),
+            v((1, size), f32),
+            v((1, size), f32),
+            dma((3,)),
             v((conv_count, parts) + chunk, bf),
             v((parts,) + chunk, bf),
             v((parts,) + chunk, bf),
@@ -778,13 +791,41 @@
             dma((2, parts)), dma((2, parts)), dma((2,)),
         ],
         compiler_params=pltpu.CompilerParams(
-            collective_id=0, has_side_effects=True, vmem_limit_bytes=60 << 20
+            collective_id=0, has_side_effects=True, vmem_limit_bytes=48 << 20
         ),
     )(
-        tile_owner.T, tile_count, gate, visible, q_gain[None], k_gain[None],
-        queries[0], d_out[0], keys, values,
-    )
-    return (att[None], dq[None], dk, dv)
+        tile_owner.T, tile_count, gate,
+        *[
+            pltpu.with_memory_space_constraint(a, pltpu.HBM)
+            for a in (
+                visible, q_gain[None], k_gain[None], queries[0], d_out[0], keys, values,
+            )
+        ],
+    )
+    return store_results(att[None], dq[None], dk, dv)
+
+
+def store_kernel(*refs):
+    count = len(refs) // 2
+    saves = [
+        pltpu.make_async_copy(src, dst, refs[-1].at[n])
+        for n, (src, dst) in enumerate(zip(refs[:count], refs[count:]))
+    ]
+    for save in saves:
+        save.start()
+    for save in saves:
+        save.wait()
+
+
+def store_results(*results):
+    return pl.pallas_call(
+        store_kernel,
+        out_shape=[jax.ShapeDtypeStruct(r.shape, r.dtype) for r in results],
+        in_specs=[pl.BlockSpec(memory_space=pltpu.VMEM)] * len(results),
+        out_specs=[pl.BlockSpec(memory_space=pltpu.HBM)] * len(results),
+        scratch_shapes=[pltpu.SemaphoreType.DMA((len(results),))],
+        compiler_params=pltpu.CompilerParams(vmem_limit_bytes=8 << 20),
+    )(*results)
 
 
 def shards(queries, keys, *rest):

time: 136 us -> 132 us (0.971)
  local copies, waits for them, and re-layouts: 5.15 us -> 0.67 us
    unnamed x10 -> x4, local copies, waits for them, and re-layouts: 5.15 us -> 0.67 us
    pallas_call x0 -> x1, Pallas kernels: none -> 1.56 us  [store_results(): pl.pallas_call(store_kernel, out_shape=[jax.ShapeDtypeStruct(r.shape, r.d...]
where the time goes in v4:
time: 132 us; the launch traced here: 131 us
  Pallas kernels  129 us (98%)
    pallas_call x1, Pallas kernels, head_shards(): pl.pallas_call(partial(head_kernel, conv_count=conv_count, seq_count=seq_...  128 us

profile of v4, /device:TPU:9, one launch (start us, length us, event | category | flops | bytes accessed | tf_op | source)
XLA Modules:
  0.0 131.4 jit_solution(5746670394029244023)
XLA Ops:
  1.3 0.0 copy-start
  1.3 0.0 copy-start.1
  1.3 0.7 copy-done
  2.0 0.0 copy-done.1
  2.0 127.9 %shard_map.129 = (bf16[128,2048]{1,0:T(8,128)(2,1)S(1)}, bf16[128,2048]{1,0:T(8,128)(2,1)S(1)}, bf16[2,208,1024]{2,1,0:T(8,128)(2,1)S(1)}, bf16[2,208,1024]{2,1,0:T(8,128)(2,1)S(1)}) custom-call(s32[2,4]{1,0:T(2,128)S(1)} %bitcast.9, s32[4]{0:T(128)S(1)} %copy-done.1, f32[1]{0:T(128)S(6)} %copy.14.gate, s32[4,512]{1,0:T(4,128)} %visible_hbm.1, ...), custom_call_target="tpu_custom_call" | custom-call | tf_op jit(solution)/shard_map/pallas_call | solution.py:749
  129.8 1.6 %shard_map.130 = (bf16[1,128,2048]{2,1,0:T(8,128)(2,1)}, bf16[1,128,2048]{2,1,0:T(8,128)(2,1)}, bf16[2,208,1024]{2,1,0:T(8,128)(2,1)}, bf16[2,208,1024]{2,1,0:T(8,128)(2,1)}) custom-call(bf16[1,128,2048]{2,1,0:T(8,128)(2,1)S(1)} %bitcast.7, bf16[1,128,2048]{2,1,0:T(8,128)(2,1)S(1)} %bitcast.8, bf16[2,208,1024]{2,1,0:T(8,128)(2,1)S(1)} %get-tuple-element.10.refs_2_, ...), custom_call_target="tpu_custom_call" | custom-call | tf_op jit(solution)/shard_map/pallas_call | solution.py:821
Async XLA Ops:
  1.3 0.7 copy-start
  1.3 0.7 copy-start.1

commit v5 on v4

--- a/solution.py
+++ b/solution.py
@@ -665,11 +665,11 @@
 
         late = n - parts // 2
 
-        @pl.when((late >= 0) & (late % 2 == 0))
+        @pl.when(late == 0)
         def _():
-            pass_back(late // 2)
-
-    passed = (parts - parts // 2 + 1) // 2
+            pass_back(0)
+
+    passed = 1
     pass_back(passed)
 
     @pl.loop(0, seq_count)

time: 132 us -> 131 us (level)
  no operation moved by 1% of the time
where the time goes in v5:
time: 131 us
  Pallas kernels  129 us (98%)
    pallas_call x1, Pallas kernels, head_shards(): pl.pallas_call(partial(head_kernel, conv_count=conv_count, seq_count=seq_...  128 us

profile of v5, /device:TPU:9, one launch (start us, length us, event | category | flops | bytes accessed | tf_op | source)
XLA Modules:
  0.0 131.3 jit_solution(12198811567201695691)
XLA Ops:
  1.3 0.0 copy-start
  1.3 0.0 copy-start.1
  1.3 0.7 copy-done
  2.0 0.0 copy-done.1
  2.0 127.8 %shard_map.129 = (bf16[128,2048]{1,0:T(8,128)(2,1)S(1)}, bf16[128,2048]{1,0:T(8,128)(2,1)S(1)}, bf16[2,208,1024]{2,1,0:T(8,128)(2,1)S(1)}, bf16[2,208,1024]{2,1,0:T(8,128)(2,1)S(1)}) custom-call(s32[2,4]{1,0:T(2,128)S(1)} %bitcast.9, s32[4]{0:T(128)S(1)} %copy-done.1, f32[1]{0:T(128)S(6)} %copy.14.gate, s32[4,512]{1,0:T(4,128)} %visible_hbm.1, ...), custom_call_target="tpu_custom_call" | custom-call | tf_op jit(solution)/shard_map/pallas_call | solution.py:749
  129.8 1.6 %shard_map.130 = (bf16[1,128,2048]{2,1,0:T(8,128)(2,1)}, bf16[1,128,2048]{2,1,0:T(8,128)(2,1)}, bf16[2,208,1024]{2,1,0:T(8,128)(2,1)}, bf16[2,208,1024]{2,1,0:T(8,128)(2,1)}) custom-call(bf16[1,128,2048]{2,1,0:T(8,128)(2,1)S(1)} %bitcast.7, bf16[1,128,2048]{2,1,0:T(8,128)(2,1)S(1)} %bitcast.8, bf16[2,208,1024]{2,1,0:T(8,128)(2,1)S(1)} %get-tuple-element.10.refs_2_, ...), custom_call_target="tpu_custom_call" | custom-call | tf_op jit(solution)/shard_map/pallas_call | solution.py:821
Async XLA Ops:
  1.3 0.7 copy-start
  1.3 0.7 copy-start.1
